TPU v7x, 32 devices: a whole 2x2x4 slice. The times are simulated.
32 devices in a mesh: dom: 8 (over y, x, core), feat: 4 (over z).
Axes of the slice: x: 2, y: 2, z: 4, core: 2. Of those that a mesh axis runs over, the one named last changes fastest.
Arguments:
- features: bfloat16 [128, 131072], P('feat', 'dom'), may hold values from -6 to 6
- seed_rows: int32 [2048], P('dom'), may hold values from 0 to 16383
- want_rows: int32 [8, 8, 128], P('dom'), may hold values from 0 to 16383
- live_counts: int32 [8, 8], P('dom'), may hold values from 1 to 128, as said below
- hop_one: int32 [15, 2048], P(None, 'dom'), may hold values from 0 to 1023, as said below
- hop_two: int32 [10, 15, 2048], P(None, None, 'dom'), may hold values from 0 to 1023, as said below
- w1_self: bfloat16 [256, 128], replicated, may hold values from -0.5 to 0.5
- w1_neigh: bfloat16 [256, 128], replicated, may hold values from -0.5 to 0.5
- b1: float32 [256], P('feat'), may hold values from -4 to 4
- w2_self: bfloat16 [256, 256], P(None, 'feat'), may hold values from -0.375 to 0.375
- w2_neigh: bfloat16 [256, 256], P(None, 'feat'), may hold values from -0.375 to 0.375
- b2: float32 [256], P('feat'), may hold values from -4 to 4
Outputs:
- embed: float32 [256, 2048], P('feat', 'dom')
Inputs may be any that keep to these rules, and one draw needn't show every extreme that they name: `want_rows`: slots at or beyond live_counts[r, o] are ignored. `live_counts`: in every draw a quarter of the owners, every fourth one from a drawn offset, receive all 128 slots from every requester. `hop_one`: each entry is o * 128 + c, a position in the buffer of the requester that holds seed s, with c < live_counts of that requester and owner o. `hop_two`: each entry is o * 128 + c, a position in the buffer of the requester that holds seed s, with c < live_counts of that requester and owner o.
All inputs are finite; a program needn't handle non-finite values.
Results may differ from a plain program's by a relative error of at most 0.00036.
Values may be sent and summed in bfloat16 or wider, within the bound.
No kernel may reach another device: no remote copies, remote signals or barrier semaphores. Data moves between devices by JAX's collectives and lax.ppermute only.
A program may use at most 64 MiB of HBM per device.

v0:
```python
import jax
import jax.numpy as jnp
from jax import lax
from jax.sharding import PartitionSpec as P

OUT = 256
FAN1 = 15
FAN2 = 10
CAP = 128


def aggregate_counts(fetched, hop_one, hop_two):
    feat_dev, slots = fetched.shape
    width = CAP * 4
    first = hop_one.reshape(1, -1)
    second = hop_two.reshape(FAN2, -1)
    columns = first.shape[1]

    def add_block(blocks, carry):
        start = blocks * width
        piece = lax.dynamic_slice_in_dim(fetched, start, width, 1)
        place = start + lax.broadcasted_iota(jnp.int32, (width, 1), 0)
        pick_one = (first == place).astype(jnp.bfloat16)
        pick_two = jnp.zeros((width, columns), jnp.bfloat16)
        for sample in range(FAN2):
            pick_two = pick_two + (second[sample : sample + 1] == place).astype(jnp.bfloat16)
        own_sum = carry[0] + jnp.dot(piece, pick_one, preferred_element_type=jnp.float32)
        mean_sum = carry[1] + jnp.dot(piece, pick_two, preferred_element_type=jnp.float32)
        return (own_sum, mean_sum)

    zeros = jnp.zeros((feat_dev, columns), jnp.float32)
    own_sum, mean_sum = lax.fori_loop(0, slots // width, add_block, (zeros, zeros))
    return (own_sum.astype(jnp.bfloat16), (mean_sum * (1.0 / FAN2)).astype(jnp.bfloat16))


def per_device(
    features,
    seed_rows,
    want_rows,
    live_counts,
    hop_one,
    hop_two,
    w1_self,
    w1_neigh,
    b1,
    w2_self,
    w2_neigh,
    b2,
):
    feat_dev = features.shape[0]
    seed_dev = seed_rows.shape[0]
    hid_dev = b1.shape[0]
    served = jnp.take(
        features,
        lax.all_to_all(want_rows, "dom", split_axis=1, concat_axis=0, tiled=True)[:, 0, :],
        axis=1,
    )
    returned = lax.all_to_all(served, "dom", split_axis=1, concat_axis=1, tiled=True)
    slot_ids = lax.broadcasted_iota(jnp.int32, (1, returned.shape[2]), 1)
    live_slots = slot_ids < live_counts[0][:, None]
    fetched = jnp.where(live_slots[None], returned, jnp.zeros((), jnp.bfloat16)).reshape(
        feat_dev, -1
    )
    x_one, m_two = aggregate_counts(fetched, hop_one, hop_two)
    x_seed = jnp.take(features, seed_rows, axis=1)
    m_one = jnp.sum(x_one.reshape(feat_dev, FAN1, seed_dev), axis=1, dtype=jnp.float32)
    m_one = (m_one * (1.0 / FAN1)).astype(jnp.bfloat16)
    selves = jnp.concatenate([x_one, x_seed], axis=1)
    means = jnp.concatenate([m_two, m_one], axis=1)
    hid_start = lax.axis_index("feat") * hid_dev
    self_rows = lax.dynamic_slice_in_dim(w1_self, hid_start, hid_dev, 0)
    neigh_rows = lax.dynamic_slice_in_dim(w1_neigh, hid_start, hid_dev, 0)
    self_part = self_rows
    neigh_part = neigh_rows
    total = jnp.dot(
        self_part,
        lax.all_gather(selves, "feat", axis=0, tiled=True),
        preferred_element_type=jnp.float32,
    )
    pre = total + jnp.dot(
        neigh_part,
        lax.all_gather(means, "feat", axis=0, tiled=True),
        preferred_element_type=jnp.float32,
    )
    hidden = jnp.maximum(pre + b1[:, None], 0.0)
    hop_cols = FAN1 * seed_dev
    h_one = hidden[:, :hop_cols]
    h_seed = hidden[:, hop_cols:]
    g_mean = jnp.sum(h_one.reshape(hid_dev, FAN1, seed_dev), axis=1) * (1.0 / FAN1)
    second_self = w2_self.astype(jnp.float32)
    second_neigh = w2_neigh.astype(jnp.float32)
    self_part = second_self
    neigh_part = second_neigh
    total = jnp.dot(
        self_part, h_seed, precision=lax.Precision.HIGHEST, preferred_element_type=jnp.float32
    )
    z_out = (
        lax.psum_scatter(
            total
            + jnp.dot(
                neigh_part,
                g_mean,
                precision=lax.Precision.HIGHEST,
                preferred_element_type=jnp.float32,
            ),
            "feat",
            scatter_dimension=0,
            tiled=True,
        )
        + b2[:, None]
    )
    square = lax.psum(jnp.sum(z_out * z_out, axis=0), "feat")
    return z_out * lax.rsqrt(square * (1.0 / OUT) + 1.0)


def solution(mesh):
    return jax.shard_map(
        per_device,
        mesh=mesh,
        in_specs=(
            P("feat", "dom"),
            P("dom"),
            P("dom", None, None),
            P("dom", None),
            P(None, "dom"),
            P(None, None, "dom"),
            P(),
            P(),
            P("feat"),
            P(None, "feat"),
            P(None, "feat"),
            P("feat"),
        ),
        out_specs=P("feat", "dom"),
        check_vma=False,
    )
```

profile of v0, /device:TPU:0, one launch (start us, length us, event | category | flops | bytes accessed | tf_op | source)
XLA Modules:
  0.0 154.2 jit_solution(16646595926999399263)
XLA Ops:
  6.5 5.3 %all-to-all-start = ((s32[1,8,128]{2,0,1:T(1,128)}), s32[1,8,128]{2,0,1:T(1,128)S(1)}, u32[]{:S(2)}, u32[]{:S(2)}) async-start(s32[1,8,128]{2,0,1:T(1,128)} %bitcast.38), calls=%async_computation | async-start | bytes 8192 | tf_op jit(solution)/shard_map/all_to_all | solution.py:55
  11.9 0.7 compare_select_fusion.2
  12.6 0.7 compare_and_fusion.1
  13.2 4.6 %copy.30 = bf16[32,16384]{0,1:T(8,128)(2,1)} copy(bf16[32,16384]{1,0:T(8,128)(2,1)} %param.14) | data formatting | bytes 2097152 | tf_op args[0]
  17.8 3.5 %gather_fusion.1 = bf16[256,32]{1,0:T(8,128)(2,1)S(1)} fusion(bf16[32,16384]{0,1:T(8,128)(2,1)} %copy.30, s32[1024]{0:T(1024)S(1)} %pad_clamp_fusion), kind=kCustom, calls=%fused_computation.1 | custom fusion | bytes 33792 | tf_op jit(solution)/shard_map/jit(_take)/gather | solution.py:65
  21.3 0.1 select_bitcast_fusion
  21.4 5.6 %gather_fusion = bf16[1024,32]{1,0:T(8,128)(2,1)S(1)} fusion(bf16[32,16384]{0,1:T(8,128)(2,1)} %copy.30, s32[1024]{0:T(1024)S(1)} %fusion.43), kind=kCustom, calls=%fused_computation | custom fusion | bytes 135168 | tf_op jit(solution)/shard_map/jit(_take)/gather | solution.py:53
  27.0 0.1 copy.31
  27.2 0.6 select_bitcast_fusion.1
  27.8 4.2 %all-to-all-start.1 = ((bf16[32,8,128]{2,0,1:T(8,128)(2,1)}), bf16[32,8,128]{2,0,1:T(8,128)(2,1)S(1)}, u32[]{:S(2)}, u32[]{:S(2)}) async-start(bf16[32,8,128]{2,0,1:T(8,128)(2,1)} %select_bitcast_fusion.1), calls=%async_computation.1 | async-start | bytes 131072 | tf_op jit(solution)/shard_map/all_to_all | solution.py:58
  32.0 0.2 all-gather.3.cloned.1.call-start
  32.3 0.1 iota_compare_fusion
  32.3 0.1 copy.34
  32.5 0.1 copy.40
  32.6 4.4 %all-to-all-done.1 = bf16[32,8,128]{2,0,1:T(8,128)(2,1)S(1)} async-done(((bf16[32,8,128]{2,0,1:T(8,128)(2,1)}), bf16[32,8,128]{2,0,1:T(8,128)(2,1)S(1)}, u32[]{:S(2)}, u32[]{:S(2)}) %all-to-all-start.1) | async-done | bytes 65568 | tf_op jit(solution)/shard_map/all_to_all | solution.py:58
  37.1 19.3 %while.16 = (s32[]{:T(128)}, f32[32,3840]{1,0:T(8,128)S(1)}, f32[32,3840]{1,0:T(8,128)S(1)}, bf16[32,1024]{1,0:T(8,128)(2,1)S(1)}, s32[1,3840]{1,0:T(1,128)S(1)}...) while((s32[]{:T(128)}, f32[32,3840]{1,0:T(8,128)S(1)}, ...), condition=%wide.region_1.2_spmd.clone, body=%wide.region_0.1_spmd.clone.sunk | while | flops 311132672 | bytes 2556086 | solution.py:32
  37.1 1.5 fusion.60
  38.6 0.4 slice_reduce_fusion.11
  39.0 7.7 %convolution_add_fusion.4 = f32[32,3840]{1,0:T(8,128)S(1)} fusion(s32[3840]{0:T(1024)S(1)} %get-tuple-element.207, s32[3840]{0:T(1024)S(1)} %get-tuple-element.208, s32[3840]{0:T(1024)S(1)} %get-tuple-element.209, s32[3840]{0:T(1024)S(1)} %get-tuple-element.210, s32[3840]{0:T(1024)S(1)} %get-tuple-element.211, s32[3840]{0:T(1024)S(1)} %get-tuple-element.212, ...), kind=kOutput, calls=%fused_computation.14.clone.1 | convolution fusion | flops 183091200 | bytes 1181701 | tf_op jit(solution)/shard_map/while/body/eval_jaxpr/dot_general | solution.py:28
  46.8 1.5 fusion.60
  48.3 0.4 slice_reduce_fusion.11
  48.7 7.7 %convolution_add_fusion.4 = f32[32,3840]{1,0:T(8,128)S(1)} fusion(s32[3840]{0:T(1024)S(1)} %get-tuple-element.207, s32[3840]{0:T(1024)S(1)} %get-tuple-element.208, s32[3840]{0:T(1024)S(1)} %get-tuple-element.209, s32[3840]{0:T(1024)S(1)} %get-tuple-element.210, s32[3840]{0:T(1024)S(1)} %get-tuple-element.211, s32[3840]{0:T(1024)S(1)} %get-tuple-element.212, ...), kind=kOutput, calls=%fused_computation.14.clone.1 | convolution fusion | flops 183091200 | bytes 1181701 | tf_op jit(solution)/shard_map/while/body/eval_jaxpr/dot_general | solution.py:28
  56.5 0.2 reshape.90
  56.7 0.7 pad_maximum_fusion
  57.4 0.0 all-gather.3.cloned.1.call-update
  57.4 0.0 all-gather.5.cloned.1.call-start
  57.5 0.1 reduce_sum.27
  57.7 0.7 pad_maximum_fusion.1
  58.4 0.0 all-gather.5.cloned.1.call-update
  58.4 0.0 reduce-scatter.4.cloned.1.call-start
  58.5 26.5 %all-gather.3.cloned.1.call-done = bf16[128,4096]{1,0:T(8,128)(2,1)} async-done(((bf16[32,4096]{1,0:T(8,128)(2,1)}), bf16[128,4096]{1,0:T(8,128)(2,1)}) %all-gather.3.cloned.1.call-update) | async-done | bytes 1048592 | tf_op jit(solution)/shard_map/all_gather | solution.py:77
  84.9 1.5 fusion.40
  86.5 27.4 %all-gather.5.cloned.1.call-done = bf16[128,4096]{1,0:T(8,128)(2,1)} async-done(((bf16[32,4096]{1,0:T(8,128)(2,1)}), bf16[128,4096]{1,0:T(8,128)(2,1)}) %all-gather.5.cloned.1.call-update) | async-done | bytes 1048592 | tf_op jit(solution)/shard_map/all_gather | solution.py:82
  113.9 1.5 fusion.33
  115.4 0.0 copy-start.5
  115.4 0.1 slice.93
  115.5 0.3 fusion.35
  115.9 0.3 reshape.89
  116.2 0.2 reduce_sum.28
  116.4 0.3 fusion.34
  116.7 0.8 copy.36
  117.5 0.0 reduce-scatter.4.cloned.1.call-update
  117.5 19.5 %reduce-scatter.4.cloned.1.call-done = f32[64,256]{1,0:T(8,128)} async-done(((f32[256,256]{1,0:T(8,128)}), f32[64,256]{1,0:T(8,128)}) %reduce-scatter.4.cloned.1.call-update) | async-done | bytes 65552
  137.1 0.9 copy.37
  138.0 0.1 multiply_reduce_fusion
  138.1 8.8 %psum.7 = f32[256]{0:T(256)S(1)} all-reduce(f32[256]{0:T(256)S(1)} %multiply_reduce_fusion), channel_id=1, replica_groups=mesh['dom'=8,'feat'=4] {'feat'}, use_global_device_ids=true, to_apply=%region_6.7 | all-reduce | flops 256 | bytes 2048 | tf_op jit(solution)/shard_map/psum | solution.py:112
  146.9 0.1 add_multiply_fusion
  147.0 0.7 copy.35
  (32 shorter events, 0.3 us)
Async XLA Ops:
  6.5 78.4 %copy-start = (bf16[256,128]{1,0:T(8,128)(2,1)S(1)}, bf16[256,128]{1,0:T(8,128)(2,1)}, u32[]{:S(2)}) copy-start(bf16[256,128]{1,0:T(8,128)(2,1)} %param.20) | copy-start | bytes 196612
  6.5 25.7 %copy-start.7 = (s32[1,8]{1,0:T(1,128)S(1)}, s32[1,8]{1,0:T(1,128)}, u32[]{:S(2)}) copy-start(s32[1,8]{1,0:T(1,128)} %param.17) | copy-start | bytes 100
  6.5 25.9 %copy-start.4 = (s32[15,256]{1,0:T(8,128)S(1)}, s32[15,256]{1,0:T(8,128)}, u32[]{:S(2)}) copy-start(s32[15,256]{1,0:T(8,128)} %param.18) | copy-start | bytes 46084
  6.5 25.9 %copy-start.1 = (s32[10,15,256]{2,1,0:T(8,128)S(1)}, s32[10,15,256]{2,1,0:T(8,128)}, u32[]{:S(2)}) copy-start(s32[10,15,256]{2,1,0:T(8,128)} %param.19) | copy-start | bytes 460804
  6.5 14.9 %all-to-all-start = ((s32[1,8,128]{2,0,1:T(1,128)}), s32[1,8,128]{2,0,1:T(1,128)S(1)}, u32[]{:S(2)}, u32[]{:S(2)}) async-start(s32[1,8,128]{2,0,1:T(1,128)} %bitcast.38), calls=%async_computation | async-start | bytes 8192 | tf_op jit(solution)/shard_map/all_to_all | solution.py:55
  27.8 9.2 %all-to-all-start.1 = ((bf16[32,8,128]{2,0,1:T(8,128)(2,1)}), bf16[32,8,128]{2,0,1:T(8,128)(2,1)S(1)}, u32[]{:S(2)}, u32[]{:S(2)}) async-start(bf16[32,8,128]{2,0,1:T(8,128)(2,1)} %select_bitcast_fusion.1), calls=%async_computation.1 | async-start | bytes 131072 | tf_op jit(solution)/shard_map/all_to_all | solution.py:58
  32.0 52.9 %all-gather.3.cloned.1.call-start = ((), (), s32[]{:S(2)}) async-start(), calls=%async_computation.3 | async-start | bytes 1310720 | tf_op jit(solution)/shard_map/all_gather | solution.py:77
  56.4 57.5 %copy-start.6 = (f32[64]{0:T(128)S(1)}, f32[64]{0:T(128)}, u32[]{:S(2)}) copy-start(f32[64]{0:T(128)} %param.22) | copy-start | bytes 772
  57.4 56.5 %all-gather.5.cloned.1.call-start = ((), (), s32[]{:S(2)}) async-start(), calls=%async_computation.4 | async-start | bytes 1310720 | tf_op jit(solution)/shard_map/all_gather | solution.py:82
  57.6 57.9 %copy-start.3 = (bf16[256,64]{0,1:T(8,128)(2,1)S(1)}, bf16[256,64]{0,1:T(8,128)(2,1)}, u32[]{:S(2)}) copy-start(bf16[256,64]{0,1:T(8,128)(2,1)} %param.23) | copy-start | bytes 98308
  58.4 78.7 %reduce-scatter.4.cloned.1.call-start = ((), (), s32[]{:S(2)}) async-start(), calls=%async_computation.5 | async-start | bytes 327680
  86.4 29.9 %copy-start.2 = (bf16[256,64]{0,1:T(8,128)(2,1)S(1)}, bf16[256,64]{0,1:T(8,128)(2,1)}, u32[]{:S(2)}) copy-start(bf16[256,64]{0,1:T(8,128)(2,1)} %param.24) | copy-start | bytes 98308
  115.4 22.6 %copy-start.5 = (f32[64]{0:T(128)S(1)}, f32[64]{0:T(128)}, u32[]{:S(2)}) copy-start(f32[64]{0:T(128)} %param.25) | copy-start | bytes 772
Sparse Core Ops, SparseCore 0:
  57.5 27.3 all-gather.2
  86.5 27.3 all-gather.4
  117.7 19.3 reduce-scatter.3
where the time goes:
time: 155 us; the launch traced here: 154 us
  waiting for transfers between devices  77.9 us (50%)
  matrix products  22 us (14%)
  local copies, waits for them, and re-layouts  17.9 us (12%)
  between operations  13.4 us (9%)
  starting transfers between devices  9.84 us (6%)
  blocking collectives  8.75 us (6%)
  other arithmetic  4.35 us (3%)
    all_gather x1, waiting for transfers between devices, per_device(): lax.all_gather(means, 'feat', axis=0, tiled=True)  27.4 us
    all_gather x1, waiting for transfers between devices, per_device(): lax.all_gather(selves, 'feat', axis=0, tiled=True)  26.5 us
    unnamed x4, waiting for transfers between devices  19.6 us
    dot_general x2, matrix products, add_block(): jnp.dot(piece, pick_two, preferred_element_type=jnp.float32)  15.4 us
    psum x1, blocking collectives, per_device(): square = lax.psum(jnp.sum(z_out * z_out, axis=0), 'feat')  8.75 us
    unnamed x22, local copies, waits for them, and re-layouts  6.56 us
    gather x2, local copies, waits for them, and re-layouts, per_device(): jnp.take(features, lax.all_to_all(want_rows, 'dom', split_axis=1, concat_...  5.73 us
    all_to_all x1, starting transfers between devices, per_device(): lax.all_to_all(want_rows, 'dom', split_axis=1, concat_axis=0, tiled=True)  5.34 us
  transfers between devices with their start and end apart: 5, of which 4 were waited for; matrix products, arithmetic and copies ran while one was open for 8% of the time, Pallas kernels for 0%

commit v1 on v0

v1 whole, which is shorter than its diff:
```python
import functools

import jax
import jax.numpy as jnp
from jax import lax
from jax.experimental import pallas as pl
from jax.experimental.pallas import tpu as pltpu
from jax.sharding import PartitionSpec as P

BF16 = jnp.bfloat16
F32 = jnp.float32
LANES = 256
PARTS = 3


def pick_columns(feats_ref, rows, emit):
    feat_dev, nodes = feats_ref.shape
    group = max(1, min(256 // feat_dev, nodes // LANES))
    for start in range(0, rows.shape[1], LANES):
        want = rows[:, start : start + LANES]
        width = want.shape[1]
        high = want >> 8
        low = want & (LANES - 1)
        place = lax.broadcasted_iota(jnp.int32, (LANES, width), 0)
        pick = jnp.where(low == place, 1.0, 0.0).astype(BF16)
        total = jnp.zeros((feat_dev, width), F32)
        for first in range(0, nodes // LANES, group):
            left = jnp.concatenate(
                [
                    feats_ref[:, (first + i) * LANES : (first + i + 1) * LANES]
                    for i in range(group)
                ],
                axis=0,
            )
            part = jnp.dot(left, pick, preferred_element_type=F32)
            for i in range(group):
                total = jnp.where(
                    high == first + i, part[i * feat_dev : (i + 1) * feat_dev], total
                )
        emit(start, total)


def seed_kernel(feats_ref, rows_ref, w2s_ref, w2n_ref, bias_ref, out_ref):
    outs, hid_dev = w2s_ref.shape
    feat_dev = feats_ref.shape[0]
    out_ref[0:outs, 0:hid_dev] = w2s_ref[...]
    out_ref[0:outs, hid_dev : 2 * hid_dev] = w2n_ref[...]

    def emit(start, value):
        halves = value.shape[1] // 128
        for i in range(halves):
            at = outs + (start // 128 + i) * feat_dev
            out_ref[at : at + feat_dev, :] = value[:, i * 128 : (i + 1) * 128].astype(BF16)

    pick_columns(feats_ref, rows_ref[...], emit)
    rest = bias_ref[...]
    base = outs + (rows_ref.shape[1] // 128) * feat_dev
    for i in range(PARTS):
        piece = rest.astype(BF16)
        rest = rest - piece.astype(F32)
        out_ref[base + 16 * i : base + 16 * (i + 1), :] = jnp.broadcast_to(piece, (16, 128))


def fetch_kernel(feat, feats_ref, rows_ref, out_ref):
    def emit(start, value):
        for i in range(value.shape[1] // 128):
            piece = value[:, i * 128 : (i + 1) * 128].astype(BF16)
            for copy in range(feat):
                out_ref[(start // 128 + i) * feat + copy] = piece

    pick_columns(feats_ref, rows_ref[...], emit)


def layer_kernel(
    feat,
    live_ref,
    fetched_ref,
    one_ref,
    two_ref,
    w1s_ref,
    w1n_ref,
    *rest,
):
    pieces = rest[:feat]
    out_ref, table, times, w1, bias_out, x_seed, x_sum, g_sum = rest[feat:]
    owners, feats, cap = fetched_ref.shape
    fan_one, seeds = one_ref.shape
    fan_two = two_ref.shape[0]
    hidden = w1s_ref.shape[0]
    hid_dev = hidden // feat
    feat_dev = feats // feat
    outs = hidden
    me = lax.axis_index("feat")

    slot = lax.broadcasted_iota(jnp.int32, (feats, cap), 1)
    for owner in range(owners):
        value = fetched_ref[owner].astype(F32)
        value = jnp.where(slot < live_ref[0, owner], value, 0.0)
        table[owner // 2, :, (owner % 2) * cap : (owner % 2 + 1) * cap] = value.astype(BF16)

    for sample in range(fan_two):
        total = jnp.zeros((fan_one, seeds), F32)
        for other in range(fan_two):
            total = total + jnp.where(two_ref[sample] == two_ref[other], 1.0, 0.0)
        times[sample] = total

    bias_base = outs + (seeds // 128) * feat_dev
    bias_one = []
    for k in range(feat):
        owner = lax.rem(me - k + feat, feat)
        rows = pl.ds(pl.multiple_of(owner * hid_dev, hid_dev), hid_dev)
        w1[k * hid_dev : (k + 1) * hid_dev, 0:feats] = w1s_ref[rows, :]
        w1[k * hid_dev : (k + 1) * hid_dev, feats : 2 * feats] = w1n_ref[rows, :]
        at = pl.multiple_of(owner * feat_dev, feat_dev)
        for i in range(seeds // 128):
            first = outs + i * feat_dev
            x_seed[pl.ds(at, feat_dev), i * 128 : (i + 1) * 128] = pieces[k][
                first : first + feat_dev, 0:128
            ]
        bias = jnp.zeros((8, 128), F32)
        for i in range(PARTS):
            bias = bias + pieces[k][bias_base + 16 * i : bias_base + 16 * (i + 1), :][0:8].astype(F32)
        column = bias.T
        bias_one.append(column[0:hid_dev, 0:1])
        bias_out[rows, :] = jnp.broadcast_to(column[hid_dev : 2 * hid_dev, 0:1], (hid_dev, 128))
    bias_one = jnp.concatenate(bias_one, axis=0)

    x_sum[...] = jnp.zeros_like(x_sum)
    g_sum[...] = jnp.zeros_like(g_sum)
    blocks = table.shape[0]
    block = table.shape[2]
    place = lax.broadcasted_iota(jnp.int32, (block, seeds), 0).astype(F32).astype(BF16)

    def low_row(value, start):
        moved = value - start
        inside = (moved >= 0) & (moved < block)
        return jnp.where(inside, moved, -1).astype(F32).astype(BF16)

    def step(j, carry):
        first = one_ref[pl.ds(j, 1), :]
        second = [two_ref[k, pl.ds(j, 1), :] for k in range(fan_two)]
        weight = [times[k, pl.ds(j, 1), :].astype(BF16) for k in range(fan_two)]
        own = jnp.zeros((feats, seeds), F32)
        mean = jnp.zeros((feats, seeds), F32)
        one = jnp.ones((), BF16)
        zero = jnp.zeros((), BF16)
        for b in range(blocks):
            pick = jnp.where(low_row(first, b * block) == place, one, zero)
            own = own + jnp.dot(table[b], pick, preferred_element_type=F32)
            count = jnp.zeros((block, seeds), BF16)
            for k in range(fan_two):
                count = jnp.where(low_row(second[k], b * block) == place, weight[k], count)
            mean = mean + jnp.dot(table[b], count, preferred_element_type=F32)
        x_sum[...] += own
        both = jnp.concatenate(
            [own.astype(BF16), (mean * (1.0 / fan_two)).astype(BF16)], axis=0
        )
        pre = jnp.dot(w1[...], both, preferred_element_type=F32)
        g_sum[...] += jnp.maximum(pre + bias_one, 0.0)
        return carry

    lax.fori_loop(0, fan_one, step, 0)

    m_one = (x_sum[...] * (1.0 / fan_one)).astype(BF16)
    both = jnp.concatenate([x_seed[...], m_one], axis=0)
    h_seed = jnp.maximum(jnp.dot(w1[...], both, preferred_element_type=F32) + bias_one, 0.0)
    g_mean = g_sum[...] * (1.0 / fan_one)
    z = jnp.zeros((outs, seeds), F32) + bias_out[:, 0:1]
    for index, value in enumerate((h_seed, g_mean)):
        w2 = jnp.concatenate(
            [
                pieces[k][0:outs, :][:, index * hid_dev : (index + 1) * hid_dev]
                for k in range(feat)
            ],
            axis=1,
        )
        high = value.astype(BF16)
        low = (value - high.astype(F32)).astype(BF16)
        z = z + jnp.dot(w2, high, preferred_element_type=F32)
        z = z + jnp.dot(w2, low, preferred_element_type=F32)
    square = jnp.sum(z * z, axis=0, keepdims=True)
    z = z * lax.rsqrt(square * (1.0 / outs) + 1.0)
    out_dev = out_ref.shape[0]
    x_sum_full = g_sum
    x_sum_full[...] = z
    out_ref[...] = x_sum_full[pl.ds(pl.multiple_of(me * out_dev, out_dev), out_dev), :]


def per_device(
    features,
    seed_rows,
    want_rows,
    live_counts,
    hop_one,
    hop_two,
    w1_self,
    w1_neigh,
    b1,
    w2_self,
    w2_neigh,
    b2,
):
    feat_dev = features.shape[0]
    seed_dev = seed_rows.shape[0]
    hid_dev = b1.shape[0]
    owners, cap = want_rows.shape[1:]
    feat = lax.axis_size("feat")
    feats = feat * feat_dev
    outs, hidden = w1_self.shape[0], w1_self.shape[0]
    vmem = pl.BlockSpec(memory_space=pltpu.VMEM)
    smem = pl.BlockSpec(memory_space=pltpu.SMEM)

    asked = lax.all_to_all(want_rows, "dom", split_axis=1, concat_axis=0, tiled=True)
    bias = jnp.concatenate([b1, b2, jnp.zeros((128 - 2 * hid_dev,), F32)])[None]
    rows = outs + (seed_dev // 128) * feat_dev + 16 * PARTS
    mine = pl.pallas_call(
        seed_kernel,
        out_shape=jax.ShapeDtypeStruct((rows, 128), BF16),
        in_specs=[vmem] * 5,
        out_specs=vmem,
        name="seed_kernel",
    )(features, seed_rows[None], w2_self, w2_neigh, bias)
    pieces = [mine] + [
        lax.ppermute(mine, "feat", [(i, (i + k) % feat) for i in range(feat)])
        for k in range(1, feat)
    ]
    served = pl.pallas_call(
        functools.partial(fetch_kernel, feat),
        out_shape=jax.ShapeDtypeStruct((owners * feat, feat_dev, cap), BF16),
        in_specs=[vmem] * 2,
        out_specs=vmem,
        name="fetch_kernel",
    )(features, asked.reshape(1, owners * cap))
    fetched = lax.all_to_all(served, ("dom", "feat"), split_axis=0, concat_axis=0, tiled=True)
    fetched = fetched.reshape(owners, feats, cap)
    return pl.pallas_call(
        functools.partial(layer_kernel, feat),
        out_shape=jax.ShapeDtypeStruct((outs // feat, seed_dev), F32),
        in_specs=[smem] + [vmem] * (5 + feat),
        out_specs=vmem,
        scratch_shapes=[
            pltpu.VMEM((owners // 2, feats, 2 * cap), BF16),
            pltpu.VMEM(hop_two.shape, F32),
            pltpu.VMEM((hidden, 2 * feats), BF16),
            pltpu.VMEM((outs, 128), F32),
            pltpu.VMEM((feats, seed_dev), BF16),
            pltpu.VMEM((feats, seed_dev), F32),
            pltpu.VMEM((outs, seed_dev), F32),
        ],
        name="layer_kernel",
    )(live_counts, fetched, hop_one, hop_two, w1_self, w1_neigh, *pieces)


def solution(mesh):
    return jax.shard_map(
        per_device,
        mesh=mesh,
        in_specs=(
            P("feat", "dom"),
            P("dom"),
            P("dom", None, None),
            P("dom", None),
            P(None, "dom"),
            P(None, None, "dom"),
            P(),
            P(),
            P("feat"),
            P(None, "feat"),
            P(None, "feat"),
            P("feat"),
        ),
        out_specs=P("feat", "dom"),
        check_vma=False,
    )
```

time: 155 us -> 49.9 us (0.32)
  waiting for transfers between devices: 77.9 us -> 5.45 us
  matrix products: 22 us -> 0 us
  Pallas kernels: 0 us -> 21.6 us
  local copies, waits for them, and re-layouts: 17.9 us -> 2.23 us
  between operations: 13.4 us -> 0.06 us
  other arithmetic: 4.35 us -> 0.58 us
    all_gather x2 -> x0, waiting for transfers between devices: 53.9 us -> none  [the longest x1 27.4 us: per_device(): lax.all_gather(means, 'feat', axis=0, tiled=True)]
    dot_general x8 -> x0, matrix products: 22 us -> none  [the longest x2 15.4 us: add_block(): jnp.dot(piece, pick_two, preferred_element_type=jnp.float32)]
    pallas_call x0 -> x3, Pallas kernels: none -> 21.6 us  [the longest x1 15.9 us: per_device(): pl.pallas_call(functools.partial(layer_kernel, feat), out_shape=jax.Shape...]
    unnamed x4 -> x0, waiting for transfers between devices: 19.6 us -> none
    all_to_all x0 -> x1, blocking collectives: none -> 9.76 us  [per_device(): lax.all_to_all(want_rows, 'dom', split_axis=1, concat_axis=0, tiled=True)]
    gather x3 -> x0, local copies, waits for them, and re-layouts: 9.19 us -> none  [the longest x2 5.73 us: per_device(): jnp.take(features, lax.all_to_all(want_rows, 'dom', split_axis=1, concat_...]
    psum x1 -> x0, blocking collectives: 8.75 us -> none  [per_device(): square = lax.psum(jnp.sum(z_out * z_out, axis=0), 'feat')]
    ppermute x0 -> x3, starting transfers between devices: none -> 5.6 us  [per_device(): lax.ppermute(mine, 'feat', [(i, (i + k) % feat) for i in range(feat)])]
  transfers between devices with their start and end apart: 5 -> 4, of which waited for: 4 -> 2; matrix products, arithmetic and copies ran while one was open for 8% -> 4% of each run, Pallas kernels for 0% -> 5%
where the time goes in v1:
time: 49.9 us; the launch traced here: 49.5 us
  Pallas kernels  21.6 us (43%)
  starting transfers between devices  9.8 us (20%)
  blocking collectives  9.76 us (20%)
  waiting for transfers between devices  5.45 us (11%)
  local copies, waits for them, and re-layouts  2.23 us (4%)
  other arithmetic  0.58 us (1%)
    pallas_call x1, Pallas kernels, per_device(): pl.pallas_call(functools.partial(layer_kernel, feat), out_shape=jax.Shape...  15.9 us
    all_to_all x1, blocking collectives, per_device(): lax.all_to_all(want_rows, 'dom', split_axis=1, concat_axis=0, tiled=True)  9.76 us
    ppermute x3, starting transfers between devices, per_device(): lax.ppermute(mine, 'feat', [(i, (i + k) % feat) for i in range(feat)])  5.6 us
    ppermute x3, waiting for transfers between devices, per_device(): lax.ppermute(mine, 'feat', [(i, (i + k) % feat) for i in range(feat)])  5.45 us
    all_to_all x1, starting transfers between devices, per_device(): lax.all_to_all(served, ('dom', 'feat'), split_axis=0, concat_axis=0, tile...  4.2 us
    pallas_call x1, Pallas kernels, per_device(): pl.pallas_call(functools.partial(fetch_kernel, feat), out_shape=jax.Shape...  3.38 us
    pallas_call x1, Pallas kernels, per_device(): pl.pallas_call(seed_kernel, out_shape=jax.ShapeDtypeStruct((rows, 128), B...  2.39 us
    unnamed x18, local copies, waits for them, and re-layouts  2.23 us
  transfers between devices with their start and end apart: 4, of which 2 were waited for; matrix products, arithmetic and copies ran while one was open for 4% of the time, Pallas kernels for 5%

profile of v1, /device:TPU:0, one launch (start us, length us, event | category | flops | bytes accessed | tf_op | source)
XLA Modules:
  0.0 49.5 jit_solution(15978049878213693892)
XLA Ops:
  0.0 9.8 %all_to_all.14 = s32[1,8,128]{2,0,1:T(1,128)} all-to-all(s32[1,8,128]{2,0,1:T(1,128)} %bitcast.8), channel_id=1, replica_groups=mesh['dom'=8,'feat'=4] {'dom'}, dimensions={1} | all-to-all | bytes 8192 | tf_op jit(solution)/shard_map/all_to_all | solution.py:213
  9.8 3.4 %fetch_kernel.1 = bf16[32,32,128]{2,1,0:T(8,128)(2,1)} custom-call(bf16[32,16384]{1,0:T(8,128)(2,1)} %feats_ref.3, s32[1,1024]{1,0:T(1,128)} %bitcast.7), custom_call_target="tpu_custom_call" | custom-call | tf_op jit(solution)/shard_map/fetch_kernel/pallas_call | solution.py:227
  13.1 0.0 copy-start.4
  13.1 4.2 %all-to-all-start.1 = ((bf16[32,32,128]{2,1,0:T(8,128)(2,1)}), bf16[32,32,128]{2,1,0:T(8,128)(2,1)S(1)}, u32[]{:S(2)}, u32[]{:S(2)}) async-start(bf16[32,32,128]{2,1,0:T(8,128)(2,1)} %fetch_kernel.1), calls=%async_computation.1 | async-start | bytes 524288 | tf_op jit(solution)/shard_map/all_to_all | solution.py:234
  17.4 0.0 copy-done.4
  17.4 0.0 copy-start.5
  17.4 0.7 %copy.16.w2s_ref = bf16[256,64]{1,0:T(8,128)(2,1)} copy(bf16[256,64]{0,1:T(8,128)(2,1)S(1)} %copy-done.4) | data formatting | bytes 65536 | tf_op args[9]
  18.1 0.0 copy-done.5
  18.1 0.0 copy-start.6
  18.1 0.0 copy-start.7
  18.1 0.7 %copy.17.w2n_ref = bf16[256,64]{1,0:T(8,128)(2,1)} copy(bf16[256,64]{0,1:T(8,128)(2,1)S(1)} %copy-done.5) | data formatting | bytes 65536 | tf_op args[10]
  18.9 0.0 copy-done.6
  18.9 0.0 copy-done.7
  18.9 0.6 %maximum_bitcast_fusion.bias_ref = f32[1,128]{1,0:T(1,128)} fusion(f32[64]{0:T(128)S(1)} %copy-done.6, f32[64]{0:T(128)S(1)} %copy-done.7), kind=kLoop, calls=%fused_computation | loop fusion | flops 128 | bytes 1024 | tf_op jit(solution)/shard_map/broadcast_in_dim | solution.py:214
  19.4 2.4 %seed_kernel.1.rest_0_ = bf16[368,128]{1,0:T(8,128)(2,1)} custom-call(bf16[32,16384]{1,0:T(8,128)(2,1)} %feats_ref.3, s32[1,256]{1,0:T(1,128)} %bitcast.9, bf16[256,64]{1,0:T(8,128)(2,1)} %copy.16.w2s_ref, bf16[256,64]{1,0:T(8,128)(2,1)} %copy.17.w2n_ref, f32[1,128]{1,0:T(1,128)} %maximum_bitcast_fusion.bias_ref), custom_call_target="tpu_custom_call" | custom-call | tf_op jit(solution)/shard_map/seed_kernel/pallas_call | solution.py:216
  21.8 1.8 %collective-permute-start = (bf16[368,128]{1,0:T(8,128)(2,1)}, bf16[368,128]{1,0:T(8,128)(2,1)S(1)}, u32[]{:S(2)}, u32[]{:S(2)}) collective-permute-start(bf16[368,128]{1,0:T(8,128)(2,1)} %seed_kernel.1.rest_0_), channel_id=1, source_target_pairs={{0,1},{1,2},{2,3},{3,0},{4,5},{5,6},{6,7},{7,4},{8,9},{9,10},{10,1... | collective-permute-start | bytes 282632 | tf_op jit(solution)/shard_map/ppermute | solution.py:224
  23.6 2.4 %collective-permute-start.1 = (bf16[368,128]{1,0:T(8,128)(2,1)}, bf16[368,128]{1,0:T(8,128)(2,1)S(1)}, u32[]{:S(2)}, u32[]{:S(2)}) collective-permute-start(bf16[368,128]{1,0:T(8,128)(2,1)} %seed_kernel.1.rest_0_), channel_id=1, source_target_pairs={{0,2},{1,3},{2,0},{3,1},{4,6},{5,7},{6,4},{7,5},{8,10},{9,11},{10,... | collective-permute-start | bytes 282632 | tf_op jit(solution)/shard_map/ppermute | solution.py:224
  26.0 1.4 %collective-permute-start.2 = (bf16[368,128]{1,0:T(8,128)(2,1)}, bf16[368,128]{1,0:T(8,128)(2,1)S(1)}, u32[]{:S(2)}, u32[]{:S(2)}) collective-permute-start(bf16[368,128]{1,0:T(8,128)(2,1)} %seed_kernel.1.rest_0_), channel_id=1, source_target_pairs={{0,3},{1,0},{2,1},{3,2},{4,7},{5,4},{6,5},{7,6},{8,11},{9,8},{10,9... | collective-permute-start | bytes 282632 | tf_op jit(solution)/shard_map/ppermute | solution.py:224
  27.4 2.0 %collective-permute-done.rest_1_ = bf16[368,128]{1,0:T(8,128)(2,1)S(1)} collective-permute-done((bf16[368,128]{1,0:T(8,128)(2,1)}, bf16[368,128]{1,0:T(8,128)(2,1)S(1)}, u32[]{:S(2)}, u32[]{:S(2)}) %collective-permute-start) | collective-permute-done | bytes 94240 | tf_op jit(solution)/shard_map/ppermute | solution.py:224
  29.5 0.0 copy-start.1
  29.5 3.4 %collective-permute-done.1.rest_2_ = bf16[368,128]{1,0:T(8,128)(2,1)S(1)} collective-permute-done((bf16[368,128]{1,0:T(8,128)(2,1)}, bf16[368,128]{1,0:T(8,128)(2,1)S(1)}, u32[]{:S(2)}, u32[]{:S(2)}) %collective-permute-start.1) | collective-permute-done | bytes 94240 | tf_op jit(solution)/shard_map/ppermute | solution.py:224
  32.9 0.0 copy-start.2
  32.9 0.0 collective-permute-done.2.rest_3_
  32.9 0.0 copy-start.3
  32.9 0.0 all-to-all-done.1
  32.9 0.0 copy-start
  32.9 0.0 copy-done.1
  32.9 0.6 %copy-done.2 = bf16[368,128]{1,0:T(8,128)(2,1)} copy-done((bf16[368,128]{1,0:T(8,128)(2,1)}, bf16[368,128]{1,0:T(8,128)(2,1)S(1)}, u32[]{:S(2)}) %copy-start.2) | copy-done | bytes 94232
  33.5 0.0 copy-done.3
  33.6 0.1 copy-done
  33.6 15.9 %layer_kernel.1 = f32[64,256]{1,0:T(8,128)} custom-call(s32[1,8]{1,0:T(1,128)} %live_ref.1, bf16[8,128,128]{2,1,0:T(8,128)(2,1)} %bitcast.6, s32[15,256]{1,0:T(8,128)} %one_ref.1, s32[10,15,256]{2,1,0:T(8,128)} %two_ref.1, bf16[256,128]{1,0:T(8,128)(2,1)} %w1s_ref.1, bf16[256,128]{1,0:T(8,128)(2,1)} %w1n_ref.1, bf16[368,128]{1,0:T(8,128)(2,1)} %seed_kernel.1.rest_0_, ...), custom_call_target="tpu_custom_call" | custom-call | tf_op jit(solution)/shard_map/layer_kernel/pallas_call | solution.py:236
Async XLA Ops:
  13.1 4.2 %copy-start.4 = (bf16[256,64]{0,1:T(8,128)(2,1)S(1)}, bf16[256,64]{0,1:T(8,128)(2,1)}, u32[]{:S(2)}) copy-start(bf16[256,64]{0,1:T(8,128)(2,1)} %param.21) | copy-start | bytes 98308
  13.1 19.8 %all-to-all-start.1 = ((bf16[32,32,128]{2,1,0:T(8,128)(2,1)}), bf16[32,32,128]{2,1,0:T(8,128)(2,1)S(1)}, u32[]{:S(2)}, u32[]{:S(2)}) async-start(bf16[32,32,128]{2,1,0:T(8,128)(2,1)} %fetch_kernel.1), calls=%async_computation.1 | async-start | bytes 524288 | tf_op jit(solution)/shard_map/all_to_all | solution.py:234
  17.4 0.8 %copy-start.5 = (bf16[256,64]{0,1:T(8,128)(2,1)S(1)}, bf16[256,64]{0,1:T(8,128)(2,1)}, u32[]{:S(2)}) copy-start(bf16[256,64]{0,1:T(8,128)(2,1)} %param.22) | copy-start | bytes 98308
  18.1 0.7 %copy-start.6 = (f32[64]{0:T(128)S(1)}, f32[64]{0:T(128)}, u32[]{:S(2)}) copy-start(f32[64]{0:T(128)} %param.23) | copy-start | bytes 772
  18.1 0.7 %copy-start.7 = (f32[64]{0:T(128)S(1)}, f32[64]{0:T(128)}, u32[]{:S(2)}) copy-start(f32[64]{0:T(128)} %param.20) | copy-start | bytes 772
  21.8 7.6 %collective-permute-start = (bf16[368,128]{1,0:T(8,128)(2,1)}, bf16[368,128]{1,0:T(8,128)(2,1)S(1)}, u32[]{:S(2)}, u32[]{:S(2)}) collective-permute-start(bf16[368,128]{1,0:T(8,128)(2,1)} %seed_kernel.1.rest_0_), channel_id=1, source_target_pairs={{0,1},{1,2},{2,3},{3,0},{4,5},{5,6},{6,7},{7,4},{8,9},{9,10},{10,1... | collective-permute-start | bytes 282632 | tf_op jit(solution)/shard_map/ppermute | solution.py:224
  23.6 9.3 %collective-permute-start.1 = (bf16[368,128]{1,0:T(8,128)(2,1)}, bf16[368,128]{1,0:T(8,128)(2,1)S(1)}, u32[]{:S(2)}, u32[]{:S(2)}) collective-permute-start(bf16[368,128]{1,0:T(8,128)(2,1)} %seed_kernel.1.rest_0_), channel_id=1, source_target_pairs={{0,2},{1,3},{2,0},{3,1},{4,6},{5,7},{6,4},{7,5},{8,10},{9,11},{10,... | collective-permute-start | bytes 282632 | tf_op jit(solution)/shard_map/ppermute | solution.py:224
  26.0 6.9 %collective-permute-start.2 = (bf16[368,128]{1,0:T(8,128)(2,1)}, bf16[368,128]{1,0:T(8,128)(2,1)S(1)}, u32[]{:S(2)}, u32[]{:S(2)}) collective-permute-start(bf16[368,128]{1,0:T(8,128)(2,1)} %seed_kernel.1.rest_0_), channel_id=1, source_target_pairs={{0,3},{1,0},{2,1},{3,2},{4,7},{5,4},{6,5},{7,6},{8,11},{9,8},{10,9... | collective-permute-start | bytes 282632 | tf_op jit(solution)/shard_map/ppermute | solution.py:224
  29.5 3.4 %copy-start.1 = (bf16[368,128]{1,0:T(8,128)(2,1)}, bf16[368,128]{1,0:T(8,128)(2,1)S(1)}, u32[]{:S(2)}) copy-start(bf16[368,128]{1,0:T(8,128)(2,1)S(1)} %collective-permute-done.rest_1_) | copy-start | bytes 282628
  32.9 0.6 %copy-start.2 = (bf16[368,128]{1,0:T(8,128)(2,1)}, bf16[368,128]{1,0:T(8,128)(2,1)S(1)}, u32[]{:S(2)}) copy-start(bf16[368,128]{1,0:T(8,128)(2,1)S(1)} %collective-permute-done.1.rest_2_) | copy-start | bytes 282628
  32.9 0.7 %copy-start.3 = (bf16[368,128]{1,0:T(8,128)(2,1)}, bf16[368,128]{1,0:T(8,128)(2,1)S(1)}, u32[]{:S(2)}) copy-start(bf16[368,128]{1,0:T(8,128)(2,1)S(1)} %collective-permute-done.2.rest_3_) | copy-start | bytes 282628
  32.9 0.8 %copy-start = (bf16[32,32,128]{2,1,0:T(8,128)(2,1)}, bf16[32,32,128]{2,1,0:T(8,128)(2,1)S(1)}, u32[]{:S(2)}) copy-start(bf16[32,32,128]{2,1,0:T(8,128)(2,1)S(1)} %all-to-all-done.1) | copy-start | bytes 786436

commit v2 on v1

v2 whole, which is shorter than its diff:
```python
import functools

import jax
import jax.numpy as jnp
from jax import lax
from jax.experimental import pallas as pl
from jax.experimental.pallas import tpu as pltpu
from jax.sharding import PartitionSpec as P


BF16 = jnp.bfloat16
F32 = jnp.float32
LANES = 256
PARTS = 3
STAGED_BYTES = 1 << 23
TILE = 16
GROUP = 3
COUNT = jnp.float8_e4m3fn


def from_where(me, k, feat):
    if feat & (feat - 1) == 0:
        return me ^ k
    return (me - k) % feat


def in_hbm(x):
    return pltpu.with_memory_space_constraint(x, pltpu.HBM)


def grant(mib, flops):
    return dict(
        compiler_params=pltpu.CompilerParams(vmem_limit_bytes=mib << 20),
        cost_estimate=pl.CostEstimate(flops=flops, bytes_accessed=1 << 20, transcendentals=0),
    )


def pick_columns(feats_ref, rows, emit):
    feat_dev, nodes = feats_ref.shape
    group = max(1, min(256 // feat_dev, nodes // LANES))
    for start in range(0, rows.shape[1], LANES):
        want = rows[:, start : start + LANES]
        width = want.shape[1]
        high = want >> 8
        low = want & (LANES - 1)
        place = lax.broadcasted_iota(jnp.int32, (LANES, width), 0)
        pick = jnp.where(low == place, 1.0, 0.0).astype(BF16)
        total = jnp.zeros((feat_dev, width), F32)
        for first in range(0, nodes // LANES, group):
            left = jnp.concatenate(
                [
                    feats_ref[:, (first + i) * LANES : (first + i + 1) * LANES]
                    for i in range(group)
                ],
                axis=0,
            )
            part = jnp.dot(left, pick, preferred_element_type=F32)
            for i in range(group):
                total = jnp.where(
                    high == first + i, part[i * feat_dev : (i + 1) * feat_dev], total
                )
        emit(start, total)


def seed_kernel(feats_ref, rows_ref, w2s_ref, w2n_ref, b1_ref, b2_ref, out_ref, near_ref):
    hid_dev, outs = w2s_ref.shape
    feat_dev = feats_ref.shape[0]
    out_ref[0:outs, 0:hid_dev] = w2s_ref[...].astype(F32).T.astype(BF16)
    out_ref[0:outs, hid_dev : 2 * hid_dev] = w2n_ref[...].astype(F32).T.astype(BF16)

    def emit(start, value):
        for i in range(value.shape[1] // 128):
            at = outs + (start // 128 + i) * feat_dev
            out_ref[at : at + feat_dev, :] = value[:, i * 128 : (i + 1) * 128].astype(BF16)

    pick_columns(feats_ref, rows_ref[...], emit)
    near_ref[...] = feats_ref[...]
    base = outs + (rows_ref.shape[1] // 128) * feat_dev
    for at, bias_ref in ((0, b1_ref), (hid_dev, b2_ref)):
        rest = jnp.broadcast_to(bias_ref[...], (16, hid_dev))
        line = lax.broadcasted_iota(jnp.int32, rest.shape, 0)
        parts = jnp.zeros_like(rest)
        for i in range(PARTS):
            piece = rest.astype(BF16).astype(F32)
            rest = rest - piece
            parts = jnp.where(line == i, piece, parts)
        out_ref[base : base + 16, at : at + hid_dev] = parts.astype(BF16)


def fetch_kernel(feat, feats_ref, rows_ref, out_ref):
    def emit(start, value):
        for i in range(value.shape[1] // 128):
            piece = value[:, i * 128 : (i + 1) * 128].astype(BF16)
            for copy in range(feat):
                out_ref[(start // 128 + i) * feat + copy] = piece

    pick_columns(feats_ref, rows_ref[...], emit)


def multiplicities(two_ref, times):
    fan_two, fan_one, seeds = two_ref.shape
    for sample in range(fan_two):
        total = jnp.zeros((fan_one, seeds), F32)
        for other in range(fan_two):
            total = total + jnp.where(two_ref[sample] == two_ref[other], 1.0, 0.0)
        times[sample] = total


def block_picks(first, second, weight, start, block):
    seeds = first.shape[1]
    place = lax.broadcasted_iota(jnp.int32, (block, seeds), 0).astype(F32).astype(BF16)

    def low_row(value):
        moved = value - start
        inside = (moved >= 0) & (moved < block)
        return jnp.where(inside, moved, -1).astype(F32).astype(BF16)

    one = jnp.ones((), BF16)
    zero = jnp.zeros((), BF16)
    pick = jnp.where(low_row(first) == place, one, zero)
    count = jnp.zeros((block, seeds), BF16)
    for value, times in zip(second, weight):
        count = jnp.where(low_row(value) == place, times, count)
    return pick, count


def pick_kernel(one_ref, two_ref, out_ref, times, made, sems):
    fan_one, seeds = one_ref.shape
    fan_two = two_ref.shape[0]
    slots = out_ref.shape[1]
    multiplicities(two_ref, times)
    line = lax.broadcasted_iota(jnp.int32, (TILE, 128), 0)
    zero = jnp.zeros((TILE, 128), BF16)
    one = jnp.ones((TILE, 128), BF16)

    def copy_of(j):
        return pltpu.make_async_copy(made.at[j], out_ref.at[j], sems.at[j])

    def step(j, carry):
        rows = [two_ref[k, pl.ds(j, 1), :] for k in range(fan_two)] + [one_ref[pl.ds(j, 1), :]]
        weights = [times[k, pl.ds(j, 1), :] for k in range(fan_two)]
        for at in range(0, seeds, 128):
            value = [
                jnp.broadcast_to(row[:, at : at + 128], (TILE, 128)).astype(jnp.int16)
                for row in rows
            ]
            times_of = [
                jnp.broadcast_to(row[:, at : at + 128], (TILE, 128)).astype(BF16)
                for row in weights
            ]
            for start in range(0, slots, 2 * TILE):
                first, second = [], []
                for half in (start, start + TILE):
                    place = (line + half).astype(jnp.int16)
                    count = zero
                    for k in range(fan_two):
                        count = jnp.where(value[k] == place, times_of[k], count)
                    first.append(jnp.where(value[fan_two] == place, one, zero))
                    second.append(count)
                for base, parts in ((0, first), (seeds, second)):
                    made[j, start : start + 2 * TILE, base + at : base + at + 128] = (
                        jnp.concatenate(parts, axis=0).astype(COUNT)
                    )
        copy_of(j).start()
        return carry

    lax.fori_loop(0, fan_one, step, 0)
    for j in range(fan_one):
        copy_of(j).wait()


def layer_kernel(feat, staged, fan_two, live_ref, fetched_ref, w1s_ref, w1n_ref, *rest):
    pieces = rest[:feat]
    picks = rest[feat : feat + (1 if staged else 2)]
    out_ref, table, staging, sems, w1, both, bias_out, x_seed, x_sum, g_sum = rest[feat + len(picks) :]
    owners, feats, cap = fetched_ref.shape
    fan_one = picks[0].shape[0]
    seeds = x_seed.shape[1]
    hidden = w1s_ref.shape[0]
    hid_dev = hidden // feat
    feat_dev = feats // feat
    outs = hidden
    me = lax.axis_index("feat")

    def copy_of(j):
        return pltpu.make_async_copy(picks[0].at[j], staging.at[j], sems.at[j])

    if staged:
        for j in range(fan_one):
            copy_of(j).start()
    slot = lax.broadcasted_iota(jnp.int32, (feats, cap), 1)
    for owner in range(owners):
        value = fetched_ref[owner].astype(F32)
        value = jnp.where(slot < live_ref[0, owner], value, 0.0)
        table[:, owner * cap : (owner + 1) * cap] = value.astype(BF16)
    if not staged:
        multiplicities(picks[1], staging)

    bias_base = outs + (seeds // 128) * feat_dev
    bias_one = []
    for k in range(feat):
        owner = from_where(me, k, feat)
        rows = pl.ds(pl.multiple_of(owner * hid_dev, hid_dev), hid_dev)
        w1[k * hid_dev : (k + 1) * hid_dev, 0:feats] = w1s_ref[rows, :]
        w1[k * hid_dev : (k + 1) * hid_dev, feats : 2 * feats] = w1n_ref[rows, :]
        at = pl.multiple_of(owner * feat_dev, feat_dev)
        for i in range(seeds // 128):
            first = outs + i * feat_dev
            x_seed[pl.ds(at, feat_dev), i * 128 : (i + 1) * 128] = pieces[k][
                first : first + feat_dev, 0:128
            ]
        parts = pieces[k][bias_base : bias_base + 16, :].astype(F32)
        bias = parts[0:1] + parts[1:2] + parts[2:3]
        column = jnp.broadcast_to(bias, (8, 128)).T
        bias_one.append(column[0:hid_dev, 0:1])
        bias_out[rows, :] = jnp.broadcast_to(column[hid_dev : 2 * hid_dev, 0:1], (hid_dev, 128))
    bias_one = jnp.concatenate(bias_one, axis=0)

    x_sum[...] = jnp.zeros_like(x_sum)

    def aggregate(j):
        if staged:
            copy_of(j).wait()
            sums = jnp.dot(table[...], staging[j], preferred_element_type=F32)
            return sums[:, 0:seeds], sums[:, seeds : 2 * seeds]
        one_ref, two_ref = picks
        first = one_ref[pl.ds(j, 1), :]
        second = [two_ref[k, pl.ds(j, 1), :] for k in range(fan_two)]
        weight = [staging[k, pl.ds(j, 1), :].astype(BF16) for k in range(fan_two)]
        own = jnp.zeros((feats, seeds), F32)
        mean = jnp.zeros((feats, seeds), F32)
        for start in range(0, owners * cap, LANES):
            pick, count = block_picks(first, second, weight, start, LANES)
            left = table[:, start : start + LANES]
            own = own + jnp.dot(left, pick, preferred_element_type=F32)
            mean = mean + jnp.dot(left, count, preferred_element_type=F32)
        return own, mean

    def step(j, carry):
        own, mean = aggregate(j)
        x_sum[...] += own
        both[j, 0:feats] = own.astype(BF16)
        both[j, feats : 2 * feats] = (mean * (1.0 / fan_two)).astype(BF16)
        return carry

    lax.fori_loop(0, fan_one, step, 0, unroll=3 if staged else 1)
    both[fan_one, 0:feats] = x_seed[...]
    both[fan_one, feats : 2 * feats] = (x_sum[...] * (1.0 / fan_one)).astype(BF16)

    g_sum[...] = jnp.zeros_like(g_sum)

    def layer(j):
        pre = jnp.dot(w1[...], both[j], preferred_element_type=F32)
        return jnp.maximum(pre + bias_one, 0.0)

    def add_layer(i, carry):
        total = layer(i * GROUP)
        for j in range(1, GROUP):
            total = total + layer(i * GROUP + j)
        g_sum[...] += total
        return carry

    lax.fori_loop(0, fan_one // GROUP, add_layer, 0)
    for j in range(fan_one // GROUP * GROUP, fan_one):
        g_sum[...] += layer(j)

    h_seed = layer(fan_one)
    g_mean = g_sum[...] * (1.0 / fan_one)
    z = jnp.zeros((outs, seeds), F32) + bias_out[:, 0:1]
    for index, value in enumerate((h_seed, g_mean)):
        w2 = jnp.concatenate(
            [
                pieces[k][0:outs, :][:, index * hid_dev : (index + 1) * hid_dev]
                for k in range(feat)
            ],
            axis=1,
        )
        high = value.astype(BF16)
        low = (value - high.astype(F32)).astype(BF16)
        z = z + jnp.dot(w2, high, preferred_element_type=F32)
        z = z + jnp.dot(w2, low, preferred_element_type=F32)
    square = jnp.sum(z * z, axis=0, keepdims=True)
    out_dev = out_ref.shape[0]
    g_sum[...] = z * lax.rsqrt(square * (1.0 / outs) + 1.0)
    out_ref[...] = g_sum[pl.ds(pl.multiple_of(me * out_dev, out_dev), out_dev), :]


def per_device(
    features,
    seed_rows,
    want_rows,
    live_counts,
    hop_one,
    hop_two,
    w1_self,
    w1_neigh,
    b1,
    w2_self,
    w2_neigh,
    b2,
):
    feat_dev = features.shape[0]
    seed_dev = seed_rows.shape[0]
    owners, cap = want_rows.shape[1:]
    feat = lax.axis_size("feat")
    feats = feat * feat_dev
    outs, hidden = w1_self.shape[0], w1_self.shape[0]
    slots = owners * cap
    fan_two, fan_one = hop_two.shape[:2]
    staged = fan_one * slots * 2 * seed_dev <= STAGED_BYTES
    vmem = pl.BlockSpec(memory_space=pltpu.VMEM)
    hbm = pl.BlockSpec(memory_space=pltpu.HBM)
    smem = pl.BlockSpec(memory_space=pltpu.SMEM)

    asked = lax.all_to_all(want_rows, "dom", split_axis=1, concat_axis=0, tiled=True)
    rows = outs + (seed_dev // 128) * feat_dev + 16
    mine, near = pl.pallas_call(
        seed_kernel,
        out_shape=[
            jax.ShapeDtypeStruct((rows, 128), BF16),
            jax.ShapeDtypeStruct(features.shape, BF16),
        ],
        in_specs=[vmem] * 6,
        out_specs=[vmem] * 2,
        name="seed_kernel",
        **grant(8, 10**9),
    )(features, *map(in_hbm, (seed_rows[None], w2_self.T, w2_neigh.T, b1[None], b2[None])))
    pieces = [mine]
    for k in range(1, feat):
        pairs = [(from_where(i, k, feat), i) for i in range(feat)]
        pieces.append(lax.ppermute(mine, "feat", pairs))
    fetch = pl.pallas_call(
        functools.partial(fetch_kernel, feat),
        out_shape=jax.ShapeDtypeStruct((owners * feat, feat_dev, cap), BF16),
        in_specs=[vmem] * 2,
        out_specs=vmem,
        name="fetch_kernel",
        **grant(8, 10**9),
    )
    served = fetch(near, asked.reshape(1, slots))
    fetched = lax.all_to_all(
        served, ("dom", "feat"), split_axis=0, concat_axis=0, tiled=True
    )
    fetched = fetched.reshape(owners, feats, cap)
    picks = (hop_one, hop_two)
    staging = pltpu.VMEM(hop_two.shape, F32)
    if staged:
        picks = (
            pl.pallas_call(
                pick_kernel,
                out_shape=pltpu.HBM((fan_one, slots, 2 * seed_dev), COUNT),
                in_specs=[vmem] * 2,
                out_specs=hbm,
                scratch_shapes=[
                    pltpu.VMEM(hop_two.shape, F32),
                    pltpu.VMEM((fan_one, slots, 2 * seed_dev), COUNT),
                    pltpu.SemaphoreType.DMA((fan_one,)),
                ],
                name="pick_kernel",
                **grant(12, 5 * 10**9),
            )(in_hbm(hop_one), in_hbm(hop_two)),
        )
        staging = pltpu.VMEM(picks[0].shape, COUNT)
    return pl.pallas_call(
        functools.partial(layer_kernel, feat, staged, fan_two),
        out_shape=jax.ShapeDtypeStruct((outs // feat, seed_dev), F32),
        in_specs=[smem] + [vmem] * (3 + feat) + [hbm if staged else vmem] * len(picks),
        out_specs=vmem,
        scratch_shapes=[
            pltpu.VMEM((feats, slots), BF16),
            staging,
            pltpu.SemaphoreType.DMA((fan_one,)),
            pltpu.VMEM((hidden, 2 * feats), BF16),
            pltpu.VMEM((fan_one + 1, 2 * feats, seed_dev), BF16),
            pltpu.VMEM((outs, 128), F32),
            pltpu.VMEM((feats, seed_dev), BF16),
            pltpu.VMEM((feats, seed_dev), F32),
            pltpu.VMEM((outs, seed_dev), F32),
        ],
        name="layer_kernel",
        **grant(24, 5 * 10**9),
    )(live_counts, fetched, w1_self, w1_neigh, *pieces, *(map(in_hbm, picks) if staged else picks))


def solution(mesh):
    return jax.shard_map(
        per_device,
        mesh=mesh,
        in_specs=(
            P("feat", "dom"),
            P("dom"),
            P("dom", None, None),
            P("dom", None),
            P(None, "dom"),
            P(None, None, "dom"),
            P(),
            P(),
            P("feat"),
            P(None, "feat"),
            P(None, "feat"),
            P("feat"),
        ),
        out_specs=P("feat", "dom"),
        check_vma=False,
    )
```

time: 49.9 us -> 42.2 us (0.85)
  blocking collectives: 9.76 us -> 0 us
  starting transfers between devices: 9.8 us -> 13.9 us
  local copies, waits for them, and re-layouts: 2.23 us -> 1.24 us
  Pallas kernels: 21.6 us -> 20.8 us
  other arithmetic: 0.58 us -> 0 us
    all_to_all x1 -> x0, blocking collectives: 9.76 us -> none  [per_device(): lax.all_to_all(want_rows, 'dom', split_axis=1, concat_axis=0, tiled=True)]
    all_to_all x0 -> x1, starting transfers between devices: none -> 5.2 us  [per_device(): lax.all_to_all(want_rows, 'dom', split_axis=1, concat_axis=0, tiled=True)]
    all_to_all x0 -> x1, waiting for transfers between devices: none -> 2.05 us  [per_device(): lax.all_to_all(want_rows, 'dom', split_axis=1, concat_axis=0, tiled=True)]
    ppermute x3, waiting for transfers between devices: 5.45 us -> 3.74 us  [per_device(): pieces.append(lax.ppermute(mine, 'feat', pairs))]
    ppermute x3, starting transfers between devices: 5.6 us -> 4.45 us  [per_device(): pieces.append(lax.ppermute(mine, 'feat', pairs))]
    unnamed x18 -> x8, local copies, waits for them, and re-layouts: 2.23 us -> 1.24 us
    pallas_call x3 -> x4, Pallas kernels: 21.6 us -> 20.8 us  [the longest x1 8.83 us: per_device(): pl.pallas_call(functools.partial(layer_kernel, feat, staged, fan_two), ou...]
    broadcast_in_dim x1 -> x0, other arithmetic: 0.58 us -> none  [per_device(): bias = jnp.concatenate([b1, b2, jnp.zeros((128 - 2 * hid_dev,), F32)])[None]]
  transfers between devices with their start and end apart: 4 -> 5, of which waited for: 2 -> 2; matrix products, arithmetic and copies ran while one was open for 4% -> 0% of each run, Pallas kernels for 5% -> 23%
where the time goes in v2:
time: 42.2 us; the launch traced here: 41.8 us
  Pallas kernels  20.8 us (49%)
  starting transfers between devices  13.9 us (33%)
  waiting for transfers between devices  5.79 us (14%)
  local copies, waits for them, and re-layouts  1.24 us (3%)
    pallas_call x1, Pallas kernels, per_device(): pl.pallas_call(functools.partial(layer_kernel, feat, staged, fan_two), ou...  8.83 us
    pallas_call x1, Pallas kernels, per_device(): pl.pallas_call(pick_kernel, out_shape=pltpu.HBM((fan_one, slots, 2 * seed...  8.48 us
    all_to_all x1, starting transfers between devices, per_device(): lax.all_to_all(want_rows, 'dom', split_axis=1, concat_axis=0, tiled=True)  5.2 us
    ppermute x3, starting transfers between devices, per_device(): pieces.append(lax.ppermute(mine, 'feat', pairs))  4.45 us
    all_to_all x1, starting transfers between devices, per_device(): lax.all_to_all(served, ('dom', 'feat'), split_axis=0, concat_axis=0, tile...  4.29 us
    ppermute x3, waiting for transfers between devices, per_device(): pieces.append(lax.ppermute(mine, 'feat', pairs))  3.74 us
    pallas_call x1, Pallas kernels, per_device(): served = fetch(near, asked.reshape(1, slots))  2.14 us
    all_to_all x1, waiting for transfers between devices, per_device(): lax.all_to_all(want_rows, 'dom', split_axis=1, concat_axis=0, tiled=True)  2.05 us
  transfers between devices with their start and end apart: 5, of which 2 were waited for; matrix products, arithmetic and copies ran while one was open for 0% of the time, Pallas kernels for 23%

profile of v2, /device:TPU:0, one launch (start us, length us, event | category | flops | bytes accessed | tf_op | source)
XLA Modules:
  0.0 41.8 jit_solution(6142143302150945229)
XLA Ops:
  0.0 5.2 %all-to-all-start = ((s32[1,8,128]{2,0,1:T(1,128)}), s32[1,8,128]{2,0,1:T(1,128)S(1)}, u32[]{:S(2)}, u32[]{:S(2)}) async-start(s32[1,8,128]{2,0,1:T(1,128)} %bitcast.10), calls=%async_computation | async-start | bytes 8192 | tf_op jit(solution)/shard_map/all_to_all | solution.py:315
  5.2 0.0 copy-start
  5.2 1.2 %copy-done = bf16[32,16384]{1,0:T(8,128)(2,1)S(1)} copy-done((bf16[32,16384]{1,0:T(8,128)(2,1)S(1)}, bf16[32,16384]{1,0:T(8,128)(2,1)}, u32[]{:S(2)}) %copy-start) | copy-done | bytes 1048600
  6.4 1.3 %seed_kernel.1 = (bf16[336,128]{1,0:T(8,128)(2,1)S(1)}, bf16[32,16384]{1,0:T(8,128)(2,1)S(1)}) custom-call(bf16[32,16384]{1,0:T(8,128)(2,1)S(1)} %copy-done, s32[1,256]{1,0:T(1,128)} %bitcast.13, bf16[64,256]{1,0:T(8,128)(2,1)} %bitcast.11, bf16[64,256]{1,0:T(8,128)(2,1)} %bitcast.12, f32[1,64]{1,0:T(1,128)} %bitcast.14, f32[1,64]{1,0:T(1,128)} %bitcast.15), custom_call_target="tpu_custom_call" | custom-call | flops 1000000000 | bytes 1048576 | tf_op jit(solution)/shard_map/seed_kernel/pallas_call | solution.py:317
  7.8 2.0 %all-to-all-done = s32[1,8,128]{2,0,1:T(1,128)S(1)} async-done(((s32[1,8,128]{2,0,1:T(1,128)}), s32[1,8,128]{2,0,1:T(1,128)S(1)}, u32[]{:S(2)}, u32[]{:S(2)}) %all-to-all-start) | async-done | bytes 4128 | tf_op jit(solution)/shard_map/all_to_all | solution.py:315
  9.8 2.1 %fetch_kernel.1 = bf16[32,32,128]{2,1,0:T(8,128)(2,1)} custom-call(bf16[32,16384]{1,0:T(8,128)(2,1)S(1)} %get-tuple-element.7.feats_ref, s32[1,1024]{1,0:T(1,128)S(1)} %bitcast.9), custom_call_target="tpu_custom_call" | custom-call | flops 1000000000 | bytes 1048576 | tf_op jit(solution)/shard_map/fetch_kernel/pallas_call | solution.py:340
  12.0 4.3 %all-to-all-start.1 = ((bf16[32,32,128]{2,1,0:T(8,128)(2,1)}), bf16[32,32,128]{2,1,0:T(8,128)(2,1)S(1)}, u32[]{:S(2)}, u32[]{:S(2)}) async-start(bf16[32,32,128]{2,1,0:T(8,128)(2,1)} %fetch_kernel.1), calls=%async_computation.1 | async-start | bytes 524288 | tf_op jit(solution)/shard_map/all_to_all | solution.py:341
  16.3 0.0 copy-start.1
  16.3 0.0 copy-start.2
  16.3 0.0 copy-start.3
  16.3 3.7 %collective-permute-start.2 = (bf16[336,128]{1,0:T(8,128)(2,1)S(1)}, bf16[336,128]{1,0:T(8,128)(2,1)S(1)}, u32[]{:S(2)}, u32[]{:S(2)}) collective-permute-start(bf16[336,128]{1,0:T(8,128)(2,1)S(1)} %get-tuple-element.8.rest_0_), channel_id=1, source_target_pairs={{3,0},{2,1},{1,2},{0,3},{7,4},{6,5},{5,6},{4,7},{11,8},{10,9},{9,1... | collective-permute-start | bytes 258056 | tf_op jit(solution)/shard_map/ppermute | solution.py:331
  20.0 0.0 collective-permute-start.1
  20.0 0.8 %collective-permute-start = (bf16[336,128]{1,0:T(8,128)(2,1)S(1)}, bf16[336,128]{1,0:T(8,128)(2,1)S(1)}, u32[]{:S(2)}, u32[]{:S(2)}) collective-permute-start(bf16[336,128]{1,0:T(8,128)(2,1)S(1)} %get-tuple-element.8.rest_0_), channel_id=1, source_target_pairs={{1,0},{0,1},{3,2},{2,3},{5,4},{4,5},{7,6},{6,7},{9,8},{8,9},{11,10... | collective-permute-start | bytes 258056 | tf_op jit(solution)/shard_map/ppermute | solution.py:331
  20.7 8.5 %pick_kernel.1.rest_4_ = f8e4m3fn[15,1024,512]{2,1,0:T(32,128)(4,1)} custom-call(s32[15,256]{1,0:T(8,128)} %one_ref.1, s32[10,15,256]{2,1,0:T(8,128)} %two_ref.1), custom_call_target="tpu_custom_call" | custom-call | flops 5000000000 | bytes 1048576 | tf_op jit(solution)/shard_map/pick_kernel/pallas_call | solution.py:349
  29.2 0.0 collective-permute-done.2.rest_3_
  29.2 3.7 %collective-permute-done.1.rest_2_ = bf16[336,128]{1,0:T(8,128)(2,1)S(1)} collective-permute-done((bf16[336,128]{1,0:T(8,128)(2,1)S(1)}, bf16[336,128]{1,0:T(8,128)(2,1)S(1)}, u32[]{:S(2)}, u32[]{:S(2)}) %collective-permute-start.1) | collective-permute-done | bytes 86048 | tf_op jit(solution)/shard_map/ppermute | solution.py:331
  33.0 0.0 collective-permute-done.rest_1_
  33.0 0.0 all-to-all-done.1
  33.0 0.0 copy-done.1
  33.0 0.0 copy-done.2
  33.0 0.0 copy-done.3
  33.0 8.8 %layer_kernel.1 = f32[64,256]{1,0:T(8,128)} custom-call(s32[1,8]{1,0:T(1,128)S(1)} %copy-done.3, bf16[8,128,128]{2,1,0:T(8,128)(2,1)S(1)} %bitcast.8, bf16[256,128]{1,0:T(8,128)(2,1)S(1)} %copy-done.1, bf16[256,128]{1,0:T(8,128)(2,1)S(1)} %copy-done.2, bf16[336,128]{1,0:T(8,128)(2,1)S(1)} %get-tuple-element.8.rest_0_, ...), custom_call_target="tpu_custom_call" | custom-call | flops 5000000000 | bytes 1048576 | tf_op jit(solution)/shard_map/layer_kernel/pallas_call | solution.py:364
Async XLA Ops:
  0.0 9.8 %all-to-all-start = ((s32[1,8,128]{2,0,1:T(1,128)}), s32[1,8,128]{2,0,1:T(1,128)S(1)}, u32[]{:S(2)}, u32[]{:S(2)}) async-start(s32[1,8,128]{2,0,1:T(1,128)} %bitcast.10), calls=%async_computation | async-start | bytes 8192 | tf_op jit(solution)/shard_map/all_to_all | solution.py:315
  5.2 1.2 %copy-start = (bf16[32,16384]{1,0:T(8,128)(2,1)S(1)}, bf16[32,16384]{1,0:T(8,128)(2,1)}, u32[]{:S(2)}) copy-start(bf16[32,16384]{1,0:T(8,128)(2,1)} %feats_ref.1) | copy-start | bytes 3145732
  12.0 21.0 %all-to-all-start.1 = ((bf16[32,32,128]{2,1,0:T(8,128)(2,1)}), bf16[32,32,128]{2,1,0:T(8,128)(2,1)S(1)}, u32[]{:S(2)}, u32[]{:S(2)}) async-start(bf16[32,32,128]{2,1,0:T(8,128)(2,1)} %fetch_kernel.1), calls=%async_computation.1 | async-start | bytes 524288 | tf_op jit(solution)/shard_map/all_to_all | solution.py:341
  16.3 16.7 %copy-start.1 = (bf16[256,128]{1,0:T(8,128)(2,1)S(1)}, bf16[256,128]{1,0:T(8,128)(2,1)}, u32[]{:S(2)}) copy-start(bf16[256,128]{1,0:T(8,128)(2,1)} %w1s_ref.1) | copy-start | bytes 196612
  16.3 16.7 %copy-start.2 = (bf16[256,128]{1,0:T(8,128)(2,1)S(1)}, bf16[256,128]{1,0:T(8,128)(2,1)}, u32[]{:S(2)}) copy-start(bf16[256,128]{1,0:T(8,128)(2,1)} %w1n_ref.1) | copy-start | bytes 196612
  16.3 16.7 %copy-start.3 = (s32[1,8]{1,0:T(1,128)S(1)}, s32[1,8]{1,0:T(1,128)}, u32[]{:S(2)}) copy-start(s32[1,8]{1,0:T(1,128)} %live_ref.1) | copy-start | bytes 100
  16.3 12.9 %collective-permute-start.2 = (bf16[336,128]{1,0:T(8,128)(2,1)S(1)}, bf16[336,128]{1,0:T(8,128)(2,1)S(1)}, u32[]{:S(2)}, u32[]{:S(2)}) collective-permute-start(bf16[336,128]{1,0:T(8,128)(2,1)S(1)} %get-tuple-element.8.rest_0_), channel_id=1, source_target_pairs={{3,0},{2,1},{1,2},{0,3},{7,4},{6,5},{5,6},{4,7},{11,8},{10,9},{9,1... | collective-permute-start | bytes 258056 | tf_op jit(solution)/shard_map/ppermute | solution.py:331
  20.0 13.0 %collective-permute-start.1 = (bf16[336,128]{1,0:T(8,128)(2,1)S(1)}, bf16[336,128]{1,0:T(8,128)(2,1)S(1)}, u32[]{:S(2)}, u32[]{:S(2)}) collective-permute-start(bf16[336,128]{1,0:T(8,128)(2,1)S(1)} %get-tuple-element.8.rest_0_), channel_id=1, source_target_pairs={{2,0},{3,1},{0,2},{1,3},{6,4},{7,5},{4,6},{5,7},{10,8},{11,9},{8,1... | collective-permute-start | bytes 258056 | tf_op jit(solution)/shard_map/ppermute | solution.py:331
  20.0 13.0 %collective-permute-start = (bf16[336,128]{1,0:T(8,128)(2,1)S(1)}, bf16[336,128]{1,0:T(8,128)(2,1)S(1)}, u32[]{:S(2)}, u32[]{:S(2)}) collective-permute-start(bf16[336,128]{1,0:T(8,128)(2,1)S(1)} %get-tuple-element.8.rest_0_), channel_id=1, source_target_pairs={{1,0},{0,1},{3,2},{2,3},{5,4},{4,5},{7,6},{6,7},{9,8},{8,9},{11,10... | collective-permute-start | bytes 258056 | tf_op jit(solution)/shard_map/ppermute | solution.py:331

commit v3 on v2

v3 whole, which is shorter than its diff:
```python
import functools

import jax
import jax.numpy as jnp
from jax import lax
from jax.experimental import pallas as pl
from jax.experimental.pallas import tpu as pltpu
from jax.sharding import PartitionSpec as P


BF16 = jnp.bfloat16
F32 = jnp.float32
LANES = 256
PARTS = 3
HELD_BYTES = 1 << 21
TILE = 32
GROUP = 3
LOADS = 4
SMALLS = 5
COUNT = jnp.float8_e4m3fn


def from_where(me, k, feat):
    if feat & (feat - 1) == 0:
        return me ^ k
    return (me - k) % feat


def unroll_of(count):
    return next(u for u in (5, 4, 3, 2, 1) if count % u == 0)


def in_hbm(x):
    return pltpu.with_memory_space_constraint(x, pltpu.HBM)


def grant(mib, flops):
    return dict(
        compiler_params=pltpu.CompilerParams(vmem_limit_bytes=mib << 20),
        cost_estimate=pl.CostEstimate(flops=flops, bytes_accessed=1 << 20, transcendentals=0),
    )


def pick_columns(feats_ref, rows, emit, ready=None):
    feat_dev, nodes = feats_ref.shape
    group = max(1, min(256 // feat_dev, nodes // LANES))
    for start in range(0, rows.shape[1], LANES):
        want = rows[:, start : start + LANES]
        width = want.shape[1]
        high = want >> 8
        low = want & (LANES - 1)
        place = lax.broadcasted_iota(jnp.int32, (LANES, width), 0)
        pick = jnp.where(low == place, 1.0, 0.0).astype(BF16)
        total = jnp.zeros((feat_dev, width), F32)
        for first in range(0, nodes // LANES, group):
            if ready is not None and start == 0:
                ready(first * LANES)
            left = jnp.concatenate(
                [
                    feats_ref[:, (first + i) * LANES : (first + i + 1) * LANES]
                    for i in range(group)
                ],
                axis=0,
            )
            part = jnp.dot(left, pick, preferred_element_type=F32)
            for i in range(group):
                total = jnp.where(
                    high == first + i, part[i * feat_dev : (i + 1) * feat_dev], total
                )
        emit(start, total)


def early_kernel(feats_ref, *rest):
    sources, (out_ref, near_ref, sems), scratch = rest[:SMALLS], rest[SMALLS : SMALLS + 3], rest[-SMALLS:]
    rows_ref, w2s_ref, w2n_ref, b1_ref, b2_ref = scratch
    hid_dev, outs = w2s_ref.shape
    feat_dev, nodes = feats_ref.shape
    loads = LOADS
    width = nodes // loads
    smalls = [
        pltpu.make_async_copy(source, scratch[i], sems.at[loads + i])
        for i, source in enumerate(sources)
    ]

    def load(i):
        part = (slice(None), pl.ds(i * width, width))
        return pltpu.make_async_copy(feats_ref.at[part], near_ref.at[part], sems.at[i])

    for copy in smalls:
        copy.start()
    for i in range(loads):
        load(i).start()
    for copy in smalls:
        copy.wait()
    out_ref[0:outs, 0:hid_dev] = w2s_ref[...].astype(F32).T.astype(BF16)
    out_ref[0:outs, hid_dev : 2 * hid_dev] = w2n_ref[...].astype(F32).T.astype(BF16)
    base = outs + (rows_ref.shape[1] // 128) * feat_dev
    for at, bias_ref in ((0, b1_ref), (hid_dev, b2_ref)):
        left = jnp.broadcast_to(bias_ref[...], (16, hid_dev))
        line = lax.broadcasted_iota(jnp.int32, left.shape, 0)
        parts = jnp.zeros_like(left)
        for i in range(PARTS):
            piece = left.astype(BF16).astype(F32)
            left = left - piece
            parts = jnp.where(line == i, piece, parts)
        out_ref[base : base + 16, at : at + hid_dev] = parts.astype(BF16)

    def emit(start, value):
        for i in range(value.shape[1] // 128):
            at = outs + (start // 128 + i) * feat_dev
            out_ref[at : at + feat_dev, :] = value[:, i * 128 : (i + 1) * 128].astype(BF16)

    def ready(column):
        if column % width == 0:
            load(column // width).wait()

    pick_columns(near_ref, rows_ref[...], emit, ready)


def fetch_kernel(feat, feats_ref, rows_ref, out_ref):
    def emit(start, value):
        for i in range(value.shape[1] // 128):
            piece = value[:, i * 128 : (i + 1) * 128].astype(BF16)
            for copy in range(feat):
                out_ref[(start // 128 + i) * feat + copy] = piece

    pick_columns(feats_ref, rows_ref[...], emit)


def multiplicities(two_ref, times):
    fan_two, fan_one, seeds = two_ref.shape
    for sample in range(fan_two):
        total = jnp.zeros((fan_one, seeds), F32)
        for other in range(fan_two):
            total = total + jnp.where(two_ref[sample] == two_ref[other], 1.0, 0.0)
        times[sample] = total


def make_counts(first, count, two_ref, times, made, out_ref=None, sems=None):
    seeds = two_ref.shape[2]
    fan_two = two_ref.shape[0]
    slots = made.shape[1]
    shape = (TILE, 128)
    i8 = jnp.int8
    line = lax.broadcasted_iota(jnp.int32, shape, 0)
    places = [(line + TILE * i).astype(i8) for i in range(128 // TILE)]
    none = jnp.full(shape, -1, i8)

    def step(j, carry):
        at_j = pl.ds(first + j, 1)
        rows = [two_ref[k, at_j, :] for k in range(fan_two)]
        weights = [times[k, at_j, :] for k in range(fan_two)]
        for at in range(0, seeds, 128):
            wide = [jnp.broadcast_to(row[:, at : at + 128], shape) for row in rows]
            low = [(value & 127).astype(i8) for value in wide]
            high = [(value >> 7).astype(i8) for value in wide]
            times_of = [
                jnp.broadcast_to(row[:, at : at + 128], shape).astype(COUNT) for row in weights
            ]
            for block in range(slots // 128):
                here = jnp.full(shape, block, i8)
                value = [jnp.where(h == here, v, none) for h, v in zip(high, low)]
                for i, place in enumerate(places):
                    total = jnp.zeros(shape, COUNT)
                    for k in range(fan_two):
                        total = jnp.where(value[k] == place, times_of[k], total)
                    start = block * 128 + i * TILE
                    made[j, start : start + TILE, at : at + 128] = total
        if out_ref is not None:
            pltpu.make_async_copy(made.at[j], out_ref.at[j], sems.at[j]).start()
        return carry

    lax.fori_loop(0, count, step, 0)


def late_kernel(held, two_ref, held_ref, out_ref, times, made, sems):
    late = out_ref.shape[0]
    multiplicities(two_ref, times)
    make_counts(held, late, two_ref, times, made, out_ref, sems)
    make_counts(0, held, two_ref, times, held_ref)
    for j in range(late):
        pltpu.make_async_copy(made.at[j], out_ref.at[j], sems.at[j]).wait()


def prep_kernel(feat, w1s_ref, w1n_ref, *rest):
    pieces = rest[:feat]
    w1, w2, x_seed, bias_one, bias_out = rest[feat:]
    hidden, feats = w1s_ref.shape
    outs = w2.shape[1]
    hid_dev = hidden // feat
    feat_dev = feats // feat
    seeds = x_seed.shape[1]
    me = lax.axis_index("feat")
    bias_base = outs + (seeds // 128) * feat_dev
    for k in range(feat):
        owner = from_where(me, k, feat)
        rows = pl.ds(pl.multiple_of(owner * hid_dev, hid_dev), hid_dev)
        here = slice(k * hid_dev, (k + 1) * hid_dev)
        w1[here, 0:feats] = w1s_ref[rows, :]
        w1[here, feats : 2 * feats] = w1n_ref[rows, :]
        at = pl.multiple_of(owner * feat_dev, feat_dev)
        for i in range(seeds // 128):
            first = outs + i * feat_dev
            x_seed[pl.ds(at, feat_dev), i * 128 : (i + 1) * 128] = pieces[k][
                first : first + feat_dev, 0:128
            ]
        parts = pieces[k][bias_base : bias_base + 16, :].astype(F32)
        bias = parts[0:1] + parts[1:2] + parts[2:3]
        column = jnp.broadcast_to(bias, (8, 128)).T
        bias_one[here, :] = jnp.broadcast_to(column[0:hid_dev, 0:1], (hid_dev, 128))
        bias_out[rows, :] = jnp.broadcast_to(column[hid_dev : 2 * hid_dev, 0:1], (hid_dev, 128))
    for index in range(2):
        w2[index] = jnp.concatenate(
            [
                pieces[k][0:outs, :][:, index * hid_dev : (index + 1) * hid_dev]
                for k in range(feat)
            ],
            axis=1,
        )


def add_bias(value, bias_ref):
    return value + jnp.concatenate([bias_ref[...]] * (value.shape[1] // 128), axis=1)


def layer_kernel(
    fan_two, live_ref, fetched_ref, one_ref, w1, w2, x_seed, bias_one, bias_out, held_ref, late_ref, *rest
):
    out_ref, table, staging, sems, both, x_sum, g_sum = rest
    owners, feats, cap = fetched_ref.shape
    fan_one, seeds = one_ref.shape
    held, late = held_ref.shape[0], late_ref.shape[0]
    outs = w2.shape[1]
    me = lax.axis_index("feat")

    def late_copy(j):
        return pltpu.make_async_copy(late_ref.at[j], staging.at[j], sems.at[j])

    for j in range(late):
        late_copy(j).start()
    slot = lax.broadcasted_iota(jnp.int32, (feats, cap), 1)
    for owner in range(owners):
        value = fetched_ref[owner].astype(F32)
        value = jnp.where(slot < live_ref[0, owner], value, 0.0)
        table[:, owner * cap : (owner + 1) * cap] = value.astype(BF16)
    x_sum[...] = jnp.zeros_like(x_sum)

    def aggregate(j, counts):
        place = lax.broadcasted_iota(jnp.int32, (owners * cap, seeds), 0)
        pick = jnp.where(one_ref[pl.ds(j, 1), :] == place, 1.0, 0.0).astype(BF16)
        own = jnp.dot(table[...], pick, preferred_element_type=F32)
        mean = jnp.dot(table[...], counts, preferred_element_type=F32)
        x_sum[...] += own
        both[j, 0:feats] = own.astype(BF16)
        both[j, feats : 2 * feats] = (mean * (1.0 / fan_two)).astype(BF16)

    def held_step(j, carry):
        aggregate(j, held_ref[j])
        return carry

    def late_step(j, carry):
        late_copy(j).wait()
        aggregate(held + j, staging[j])
        return carry

    lax.fori_loop(0, held, held_step, 0, unroll=unroll_of(held))
    lax.fori_loop(0, late, late_step, 0, unroll=unroll_of(late))
    both[fan_one, 0:feats] = x_seed[...]
    both[fan_one, feats : 2 * feats] = (x_sum[...] * (1.0 / fan_one)).astype(BF16)

    g_sum[...] = jnp.zeros_like(g_sum)

    def layer(j):
        pre = jnp.dot(w1[...], both[j], preferred_element_type=F32)
        return jnp.maximum(add_bias(pre, bias_one), 0.0)

    def add_layer(i, carry):
        total = layer(i * GROUP)
        for j in range(1, GROUP):
            total = total + layer(i * GROUP + j)
        g_sum[...] += total
        return carry

    lax.fori_loop(0, fan_one // GROUP, add_layer, 0)
    for j in range(fan_one // GROUP * GROUP, fan_one):
        g_sum[...] += layer(j)

    z = add_bias(jnp.zeros((outs, seeds), F32), bias_out)
    for index, value in enumerate((layer(fan_one), g_sum[...] * (1.0 / fan_one))):
        high = value.astype(BF16)
        low = (value - high.astype(F32)).astype(BF16)
        z = z + jnp.dot(w2[index], high, preferred_element_type=F32)
        z = z + jnp.dot(w2[index], low, preferred_element_type=F32)
    square = jnp.sum(z * z, axis=0, keepdims=True)
    out_dev = out_ref.shape[0]
    g_sum[...] = z * lax.rsqrt(square * (1.0 / outs) + 1.0)
    out_ref[...] = g_sum[pl.ds(pl.multiple_of(me * out_dev, out_dev), out_dev), :]


def per_device(
    features,
    seed_rows,
    want_rows,
    live_counts,
    hop_one,
    hop_two,
    w1_self,
    w1_neigh,
    b1,
    w2_self,
    w2_neigh,
    b2,
):
    feat_dev = features.shape[0]
    seed_dev = seed_rows.shape[0]
    owners, cap = want_rows.shape[1:]
    feat = lax.axis_size("feat")
    feats = feat * feat_dev
    outs, hidden = w1_self.shape[0], w1_self.shape[0]
    slots = owners * cap
    fan_two, fan_one = hop_two.shape[:2]
    vmem = pl.BlockSpec(memory_space=pltpu.VMEM)
    hbm = pl.BlockSpec(memory_space=pltpu.HBM)
    smem = pl.BlockSpec(memory_space=pltpu.SMEM)

    asked = lax.all_to_all(want_rows, "dom", split_axis=1, concat_axis=0, tiled=True)
    rows = outs + (seed_dev // 128) * feat_dev + 16
    held = max(1, min(fan_one - 1, HELD_BYTES // (slots * seed_dev)))
    late = fan_one - held
    two_vmem = pltpu.VMEM(hop_two.shape, F32)
    smalls = (seed_rows[None], w2_self.T, w2_neigh.T, b1[None], b2[None])
    mine, near = pl.pallas_call(
        early_kernel,
        out_shape=[pltpu.VMEM((rows, 128), BF16), pltpu.VMEM(features.shape, BF16)],
        in_specs=[hbm] * (1 + SMALLS),
        out_specs=[vmem] * 2,
        scratch_shapes=[pltpu.SemaphoreType.DMA((LOADS + SMALLS,))]
        + [pltpu.VMEM(x.shape, x.dtype) for x in smalls],
        name="early_kernel",
        **grant(8, 10**9),
    )(*map(in_hbm, (features,) + smalls))
    pieces = [mine]
    for k in range(1, feat):
        pairs = [(from_where(i, k, feat), i) for i in range(feat)]
        pieces.append(lax.ppermute(mine, "feat", pairs))
    fetch = pl.pallas_call(
        functools.partial(fetch_kernel, feat),
        out_shape=pltpu.VMEM((owners * feat, feat_dev, cap), BF16),
        in_specs=[vmem] * 2,
        out_specs=vmem,
        name="fetch_kernel",
        **grant(8, 10**9),
    )
    served = fetch(near, asked.reshape(1, slots))
    fetched = lax.all_to_all(
        served, ("dom", "feat"), split_axis=0, concat_axis=0, tiled=True
    )
    fetched = fetched.reshape(owners, feats, cap)
    block = (slots, seed_dev)
    staging = pltpu.VMEM((late,) + block, COUNT)
    held_counts, late_counts = pl.pallas_call(
        functools.partial(late_kernel, held),
        out_shape=[pltpu.VMEM((held,) + block, COUNT), pltpu.HBM((late,) + block, COUNT)],
        in_specs=[vmem],
        out_specs=[vmem, hbm],
        scratch_shapes=[two_vmem, staging, pltpu.SemaphoreType.DMA((late,))],
        name="late_kernel",
        **grant(16, 5 * 10**9),
    )(in_hbm(hop_two))
    prep = pl.pallas_call(
        functools.partial(prep_kernel, feat),
        out_shape=[
            pltpu.VMEM((hidden, 2 * feats), BF16),
            pltpu.VMEM((2, outs, hidden), BF16),
            pltpu.VMEM((feats, seed_dev), BF16),
            pltpu.VMEM((hidden, 128), F32),
            pltpu.VMEM((outs, 128), F32),
        ],
        in_specs=[vmem] * (2 + feat),
        out_specs=[vmem] * 5,
        name="prep_kernel",
        **grant(8, 10**9),
    )
    ready = prep(*map(in_hbm, (w1_self, w1_neigh)), *pieces)
    return pl.pallas_call(
        functools.partial(layer_kernel, fan_two),
        out_shape=jax.ShapeDtypeStruct((outs // feat, seed_dev), F32),
        in_specs=[smem] + [vmem] * 8 + [hbm],
        out_specs=vmem,
        scratch_shapes=[
            pltpu.VMEM((feats, slots), BF16),
            staging,
            pltpu.SemaphoreType.DMA((late,)),
            pltpu.VMEM((fan_one + 1, 2 * feats, seed_dev), BF16),
            pltpu.VMEM((feats, seed_dev), F32),
            pltpu.VMEM((outs, seed_dev), F32),
        ],
        name="layer_kernel",
        **grant(24, 5 * 10**9),
    )(live_counts, fetched, hop_one, *ready, held_counts, in_hbm(late_counts))


def solution(mesh):
    return jax.shard_map(
        per_device,
        mesh=mesh,
        in_specs=(
            P("feat", "dom"),
            P("dom"),
            P("dom", None, None),
            P("dom", None),
            P(None, "dom"),
            P(None, None, "dom"),
            P(),
            P(),
            P("feat"),
            P(None, "feat"),
            P(None, "feat"),
            P("feat"),
        ),
        out_specs=P("feat", "dom"),
        check_vma=False,
    )
```

time: 42.2 us -> 37.6 us (0.89)
  waiting for transfers between devices: 5.79 us -> 2.73 us
  Pallas kernels: 20.8 us -> 18.5 us
  starting transfers between devices: 13.9 us -> 16 us
  local copies, waits for them, and re-layouts: 1.24 us -> 0.01 us
    ppermute x3, waiting for transfers between devices: 3.74 us -> 0.01 us  [per_device(): pieces.append(lax.ppermute(mine, 'feat', pairs))]
    all_to_all x1, waiting for transfers between devices: 0.01 us -> 2.72 us  [per_device(): lax.all_to_all(served, ('dom', 'feat'), split_axis=0, concat_axis=0, tile...]
    pallas_call x3 -> x4, Pallas kernels: 18.6 us -> 16.3 us  [the longest x1 6.85 us: per_device(): pl.pallas_call(functools.partial(layer_kernel, fan_two), out_shape=jax.Sh...]
    all_to_all x1, starting transfers between devices: 4.29 us -> 6.34 us  [per_device(): lax.all_to_all(served, ('dom', 'feat'), split_axis=0, concat_axis=0, tile...]
    all_to_all x1, waiting for transfers between devices: 2.05 us -> 0.01 us  [per_device(): lax.all_to_all(want_rows, 'dom', split_axis=1, concat_axis=0, tiled=True)]
    unnamed x8 -> x4, local copies, waits for them, and re-layouts: 1.24 us -> 0.01 us
  transfers between devices with their start and end apart: 5 -> 5, of which waited for: 2 -> 1; matrix products, arithmetic and copies ran while one was open for 0% -> 0% of each run, Pallas kernels for 23% -> 31%
where the time goes in v3:
time: 37.6 us; the launch traced here: 37.3 us
  Pallas kernels  18.5 us (49%)
  starting transfers between devices  16 us (43%)
  waiting for transfers between devices  2.73 us (7%)
    pallas_call x1, Pallas kernels, per_device(): pl.pallas_call(functools.partial(layer_kernel, fan_two), out_shape=jax.Sh...  6.85 us
    all_to_all x1, starting transfers between devices, per_device(): lax.all_to_all(served, ('dom', 'feat'), split_axis=0, concat_axis=0, tile...  6.34 us
    pallas_call x1, Pallas kernels, per_device(): pl.pallas_call(functools.partial(late_kernel, held), out_shape=[pltpu.VME...  6.24 us
    all_to_all x1, starting transfers between devices, per_device(): lax.all_to_all(want_rows, 'dom', split_axis=1, concat_axis=0, tiled=True)  5.2 us
    ppermute x3, starting transfers between devices, per_device(): pieces.append(lax.ppermute(mine, 'feat', pairs))  4.45 us
    all_to_all x1, waiting for transfers between devices, per_device(): lax.all_to_all(served, ('dom', 'feat'), split_axis=0, concat_axis=0, tile...  2.72 us
    pallas_call x1, Pallas kernels, per_device(): served = fetch(near, asked.reshape(1, slots))  2.18 us
    pallas_call x1, Pallas kernels, per_device(): pl.pallas_call(early_kernel, out_shape=[pltpu.VMEM((rows, 128), BF16), pl...  2.06 us
  transfers between devices with their start and end apart: 5, of which 1 were waited for; matrix products, arithmetic and copies ran while one was open for 0% of the time, Pallas kernels for 31%

profile of v3, /device:TPU:0, one launch (start us, length us, event | category | flops | bytes accessed | tf_op | source)
XLA Modules:
  0.0 37.3 jit_solution(16667143250421798598)
XLA Ops:
  0.0 5.2 %all-to-all-start = ((s32[1,8,128]{2,0,1:T(1,128)}), s32[1,8,128]{2,0,1:T(1,128)S(1)}, u32[]{:S(2)}, u32[]{:S(2)}) async-start(s32[1,8,128]{2,0,1:T(1,128)} %bitcast.10), calls=%async_computation | async-start | bytes 8192 | tf_op jit(solution)/shard_map/all_to_all | solution.py:326
  5.2 2.1 %early_kernel.1 = (bf16[336,128]{1,0:T(8,128)(2,1)S(1)}, bf16[32,16384]{1,0:T(8,128)(2,1)S(1)}) custom-call(bf16[32,16384]{1,0:T(8,128)(2,1)} %feats_ref.1, s32[1,256]{1,0:T(1,128)} %bitcast.13, bf16[64,256]{1,0:T(8,128)(2,1)} %bitcast.11, bf16[64,256]{1,0:T(8,128)(2,1)} %bitcast.12, f32[1,64]{1,0:T(1,128)} %bitcast.14, f32[1,64]{1,0:T(1,128)} %bitcast.15), custom_call_target="tpu_custom_call" | custom-call | flops 1000000000 | bytes 1048576 | tf_op jit(solution)/shard_map/early_kernel/pallas_call | solution.py:332
  7.3 3.7 %collective-permute-start.2 = (bf16[336,128]{1,0:T(8,128)(2,1)S(1)}, bf16[336,128]{1,0:T(8,128)(2,1)S(1)}, u32[]{:S(2)}, u32[]{:S(2)}) collective-permute-start(bf16[336,128]{1,0:T(8,128)(2,1)S(1)} %get-tuple-element.15.rest_0_), channel_id=1, source_target_pairs={{3,0},{2,1},{1,2},{0,3},{7,4},{6,5},{5,6},{4,7},{11,8},{10,9},{9,1... | collective-permute-start | bytes 258056 | tf_op jit(solution)/shard_map/ppermute | solution.py:345
  10.9 0.0 collective-permute-start.1
  10.9 0.8 %collective-permute-start = (bf16[336,128]{1,0:T(8,128)(2,1)S(1)}, bf16[336,128]{1,0:T(8,128)(2,1)S(1)}, u32[]{:S(2)}, u32[]{:S(2)}) collective-permute-start(bf16[336,128]{1,0:T(8,128)(2,1)S(1)} %get-tuple-element.15.rest_0_), channel_id=1, source_target_pairs={{1,0},{0,1},{3,2},{2,3},{5,4},{4,5},{7,6},{6,7},{9,8},{8,9},{11,10... | collective-permute-start | bytes 258056 | tf_op jit(solution)/shard_map/ppermute | solution.py:345
  11.7 0.0 all-to-all-done
  11.7 2.2 %fetch_kernel.1 = bf16[32,32,128]{2,1,0:T(8,128)(2,1)} custom-call(bf16[32,16384]{1,0:T(8,128)(2,1)S(1)} %get-tuple-element.14.feats_ref, s32[1,1024]{1,0:T(1,128)S(1)} %bitcast.9), custom_call_target="tpu_custom_call" | custom-call | flops 1000000000 | bytes 1048576 | tf_op jit(solution)/shard_map/fetch_kernel/pallas_call | solution.py:354
  13.9 6.3 %all-to-all-start.1 = ((bf16[32,32,128]{2,1,0:T(8,128)(2,1)}), bf16[32,32,128]{2,1,0:T(8,128)(2,1)S(1)}, u32[]{:S(2)}, u32[]{:S(2)}) async-start(bf16[32,32,128]{2,1,0:T(8,128)(2,1)} %fetch_kernel.1), calls=%async_computation.1 | async-start | bytes 524288 | tf_op jit(solution)/shard_map/all_to_all | solution.py:355
  20.2 6.2 %late_kernel.1 = (f8e4m3fn[8,1024,256]{2,1,0:T(32,128)(4,1)S(1)}, f8e4m3fn[7,1024,256]{2,1,0:T(32,128)(4,1)}) custom-call(s32[10,15,256]{2,1,0:T(8,128)} %two_ref.1), custom_call_target="tpu_custom_call" | custom-call | flops 5000000000 | bytes 1048576 | tf_op jit(solution)/shard_map/late_kernel/pallas_call | solution.py:361
  26.5 0.0 copy-start
  26.5 0.0 copy-start.1
  26.5 0.0 collective-permute-done.2.rest_3_
  26.5 0.0 collective-permute-done.1.rest_2_
  26.5 0.0 collective-permute-done.rest_1_
  26.6 1.2 %prep_kernel.1 = (bf16[256,256]{1,0:T(8,128)(2,1)S(1)}, bf16[2,256,256]{2,1,0:T(8,128)(2,1)S(1)}, bf16[128,256]{1,0:T(8,128)(2,1)S(1)}, f32[256,128]{1,0:T(8,128)S(1)}, f32[256,128]{1,0:T(8,128)S(1)}) custom-call(bf16[256,128]{1,0:T(8,128)(2,1)} %w1s_ref.1, bf16[256,128]{1,0:T(8,128)(2,1)} %w1n_ref.1, bf16[336,128]{1,0:T(8,128)(2,1)S(1)} %get-tuple-element.15.rest_0_, ...), custom_call_target="tpu_custom_call" | custom-call | flops 1000000000 | bytes 1048576 | tf_op jit(solution)/shard_map/prep_kernel/pallas_call | solution.py:384
  27.8 2.7 %all-to-all-done.1 = bf16[32,32,128]{2,1,0:T(8,128)(2,1)S(1)} async-done(((bf16[32,32,128]{2,1,0:T(8,128)(2,1)}), bf16[32,32,128]{2,1,0:T(8,128)(2,1)S(1)}, u32[]{:S(2)}, u32[]{:S(2)}) %all-to-all-start.1) | async-done | bytes 262176 | tf_op jit(solution)/shard_map/all_to_all | solution.py:355
  30.5 0.0 copy-done
  30.5 0.0 copy-done.1
  30.5 6.9 %layer_kernel.1 = f32[64,256]{1,0:T(8,128)} custom-call(s32[1,8]{1,0:T(1,128)S(1)} %copy-done.1, bf16[8,128,128]{2,1,0:T(8,128)(2,1)S(1)} %bitcast.8, s32[15,256]{1,0:T(8,128)S(1)} %copy-done, bf16[256,256]{1,0:T(8,128)(2,1)S(1)} %get-tuple-element.16.w1, bf16[2,256,256]{2,1,0:T(8,128)(2,1)S(1)} %get-tuple-element.17.w2, ...), custom_call_target="tpu_custom_call" | custom-call | flops 5000000000 | bytes 1048576 | tf_op jit(solution)/shard_map/layer_kernel/pallas_call | solution.py:385
Async XLA Ops:
  0.0 11.7 %all-to-all-start = ((s32[1,8,128]{2,0,1:T(1,128)}), s32[1,8,128]{2,0,1:T(1,128)S(1)}, u32[]{:S(2)}, u32[]{:S(2)}) async-start(s32[1,8,128]{2,0,1:T(1,128)} %bitcast.10), calls=%async_computation | async-start | bytes 8192 | tf_op jit(solution)/shard_map/all_to_all | solution.py:326
  7.3 19.3 %collective-permute-start.2 = (bf16[336,128]{1,0:T(8,128)(2,1)S(1)}, bf16[336,128]{1,0:T(8,128)(2,1)S(1)}, u32[]{:S(2)}, u32[]{:S(2)}) collective-permute-start(bf16[336,128]{1,0:T(8,128)(2,1)S(1)} %get-tuple-element.15.rest_0_), channel_id=1, source_target_pairs={{3,0},{2,1},{1,2},{0,3},{7,4},{6,5},{5,6},{4,7},{11,8},{10,9},{9,1... | collective-permute-start | bytes 258056 | tf_op jit(solution)/shard_map/ppermute | solution.py:345
  10.9 15.6 %collective-permute-start.1 = (bf16[336,128]{1,0:T(8,128)(2,1)S(1)}, bf16[336,128]{1,0:T(8,128)(2,1)S(1)}, u32[]{:S(2)}, u32[]{:S(2)}) collective-permute-start(bf16[336,128]{1,0:T(8,128)(2,1)S(1)} %get-tuple-element.15.rest_0_), channel_id=1, source_target_pairs={{2,0},{3,1},{0,2},{1,3},{6,4},{7,5},{4,6},{5,7},{10,8},{11,9},{8,1... | collective-permute-start | bytes 258056 | tf_op jit(solution)/shard_map/ppermute | solution.py:345
  10.9 15.6 %collective-permute-start = (bf16[336,128]{1,0:T(8,128)(2,1)S(1)}, bf16[336,128]{1,0:T(8,128)(2,1)S(1)}, u32[]{:S(2)}, u32[]{:S(2)}) collective-permute-start(bf16[336,128]{1,0:T(8,128)(2,1)S(1)} %get-tuple-element.15.rest_0_), channel_id=1, source_target_pairs={{1,0},{0,1},{3,2},{2,3},{5,4},{4,5},{7,6},{6,7},{9,8},{8,9},{11,10... | collective-permute-start | bytes 258056 | tf_op jit(solution)/shard_map/ppermute | solution.py:345
  13.9 16.6 %all-to-all-start.1 = ((bf16[32,32,128]{2,1,0:T(8,128)(2,1)}), bf16[32,32,128]{2,1,0:T(8,128)(2,1)S(1)}, u32[]{:S(2)}, u32[]{:S(2)}) async-start(bf16[32,32,128]{2,1,0:T(8,128)(2,1)} %fetch_kernel.1), calls=%async_computation.1 | async-start | bytes 524288 | tf_op jit(solution)/shard_map/all_to_all | solution.py:355
  26.5 4.0 %copy-start = (s32[15,256]{1,0:T(8,128)S(1)}, s32[15,256]{1,0:T(8,128)}, u32[]{:S(2)}) copy-start(s32[15,256]{1,0:T(8,128)} %one_ref.1) | copy-start | bytes 46084
  26.5 4.0 %copy-start.1 = (s32[1,8]{1,0:T(1,128)S(1)}, s32[1,8]{1,0:T(1,128)}, u32[]{:S(2)}) copy-start(s32[1,8]{1,0:T(1,128)} %live_ref.1) | copy-start | bytes 100

commit v4 on v3

--- a/solution.py
+++ b/solution.py
@@ -14,7 +14,6 @@
 PARTS = 3
 HELD_BYTES = 1 << 21
 TILE = 32
-GROUP = 3
 LOADS = 4
 SMALLS = 5
 COUNT = jnp.float8_e4m3fn
@@ -24,10 +23,6 @@
     if feat & (feat - 1) == 0:
         return me ^ k
     return (me - k) % feat
-
-
-def unroll_of(count):
-    return next(u for u in (5, 4, 3, 2, 1) if count % u == 0)
 
 
 def in_hbm(x):
@@ -247,43 +242,31 @@
 
     def aggregate(j, counts):
         place = lax.broadcasted_iota(jnp.int32, (owners * cap, seeds), 0)
-        pick = jnp.where(one_ref[pl.ds(j, 1), :] == place, 1.0, 0.0).astype(BF16)
+        pick = jnp.where(one_ref[j : j + 1, :] == place, 1.0, 0.0).astype(BF16)
         own = jnp.dot(table[...], pick, preferred_element_type=F32)
         mean = jnp.dot(table[...], counts, preferred_element_type=F32)
         x_sum[...] += own
         both[j, 0:feats] = own.astype(BF16)
         both[j, feats : 2 * feats] = (mean * (1.0 / fan_two)).astype(BF16)
 
-    def held_step(j, carry):
+    for j in range(held - 1):
         aggregate(j, held_ref[j])
-        return carry
-
-    def late_step(j, carry):
+    for j in range(late):
         late_copy(j).wait()
+    aggregate(held - 1, held_ref[held - 1])
+    for j in range(late):
         aggregate(held + j, staging[j])
-        return carry
-
-    lax.fori_loop(0, held, held_step, 0, unroll=unroll_of(held))
-    lax.fori_loop(0, late, late_step, 0, unroll=unroll_of(late))
     both[fan_one, 0:feats] = x_seed[...]
     both[fan_one, feats : 2 * feats] = (x_sum[...] * (1.0 / fan_one)).astype(BF16)
-
-    g_sum[...] = jnp.zeros_like(g_sum)
 
     def layer(j):
         pre = jnp.dot(w1[...], both[j], preferred_element_type=F32)
         return jnp.maximum(add_bias(pre, bias_one), 0.0)
 
-    def add_layer(i, carry):
-        total = layer(i * GROUP)
-        for j in range(1, GROUP):
-            total = total + layer(i * GROUP + j)
-        g_sum[...] += total
-        return carry
-
-    lax.fori_loop(0, fan_one // GROUP, add_layer, 0)
-    for j in range(fan_one // GROUP * GROUP, fan_one):
-        g_sum[...] += layer(j)
+    total = layer(0)
+    for j in range(1, fan_one):
+        total = total + layer(j)
+    g_sum[...] = total
 
     z = add_bias(jnp.zeros((outs, seeds), F32), bias_out)
     for index, value in enumerate((layer(fan_one), g_sum[...] * (1.0 / fan_one))):

time: 37.6 us -> 35.8 us (0.952)
  Pallas kernels: 18.5 us -> 16.7 us
    pallas_call x1, Pallas kernels: 6.85 us -> 5 us  [per_device(): pl.pallas_call(functools.partial(layer_kernel, fan_two), out_shape=jax.Sh...]
  transfers between devices with their start and end apart: 5 -> 5, of which waited for: 1 -> 1; matrix products, arithmetic and copies ran while one was open for 0% -> 0% of each run, Pallas kernels for 31% -> 33%
where the time goes in v4:
time: 35.8 us; the launch traced here: 35.5 us
  Pallas kernels  16.7 us (47%)
  starting transfers between devices  16 us (45%)
  waiting for transfers between devices  2.73 us (8%)
    all_to_all x1, starting transfers between devices, per_device(): lax.all_to_all(served, ('dom', 'feat'), split_axis=0, concat_axis=0, tile...  6.34 us
    pallas_call x1, Pallas kernels, per_device(): pl.pallas_call(functools.partial(late_kernel, held), out_shape=[pltpu.VME...  6.24 us
    all_to_all x1, starting transfers between devices, per_device(): lax.all_to_all(want_rows, 'dom', split_axis=1, concat_axis=0, tiled=True)  5.2 us
    pallas_call x1, Pallas kernels, per_device(): pl.pallas_call(functools.partial(layer_kernel, fan_two), out_shape=jax.Sh...  5 us
    ppermute x3, starting transfers between devices, per_device(): pieces.append(lax.ppermute(mine, 'feat', pairs))  4.45 us
    all_to_all x1, waiting for transfers between devices, per_device(): lax.all_to_all(served, ('dom', 'feat'), split_axis=0, concat_axis=0, tile...  2.72 us
    pallas_call x1, Pallas kernels, per_device(): served = fetch(near, asked.reshape(1, slots))  2.18 us
    pallas_call x1, Pallas kernels, per_device(): pl.pallas_call(early_kernel, out_shape=[pltpu.VMEM((rows, 128), BF16), pl...  2.06 us
  transfers between devices with their start and end apart: 5, of which 1 were waited for; matrix products, arithmetic and copies ran while one was open for 0% of the time, Pallas kernels for 33%

profile of v4, /device:TPU:0, one launch (start us, length us, event | category | flops | bytes accessed | tf_op | source)
XLA Modules:
  0.0 35.5 jit_solution(10568468305325127678)
XLA Ops:
  0.0 5.2 %all-to-all-start = ((s32[1,8,128]{2,0,1:T(1,128)}), s32[1,8,128]{2,0,1:T(1,128)S(1)}, u32[]{:S(2)}, u32[]{:S(2)}) async-start(s32[1,8,128]{2,0,1:T(1,128)} %bitcast.10), calls=%async_computation | async-start | bytes 8192 | tf_op jit(solution)/shard_map/all_to_all | solution.py:309
  5.2 2.1 %early_kernel.1 = (bf16[336,128]{1,0:T(8,128)(2,1)S(1)}, bf16[32,16384]{1,0:T(8,128)(2,1)S(1)}) custom-call(bf16[32,16384]{1,0:T(8,128)(2,1)} %feats_ref.1, s32[1,256]{1,0:T(1,128)} %bitcast.13, bf16[64,256]{1,0:T(8,128)(2,1)} %bitcast.11, bf16[64,256]{1,0:T(8,128)(2,1)} %bitcast.12, f32[1,64]{1,0:T(1,128)} %bitcast.14, f32[1,64]{1,0:T(1,128)} %bitcast.15), custom_call_target="tpu_custom_call" | custom-call | flops 1000000000 | bytes 1048576 | tf_op jit(solution)/shard_map/early_kernel/pallas_call | solution.py:315
  7.3 3.7 %collective-permute-start.2 = (bf16[336,128]{1,0:T(8,128)(2,1)S(1)}, bf16[336,128]{1,0:T(8,128)(2,1)S(1)}, u32[]{:S(2)}, u32[]{:S(2)}) collective-permute-start(bf16[336,128]{1,0:T(8,128)(2,1)S(1)} %get-tuple-element.15.rest_0_), channel_id=1, source_target_pairs={{3,0},{2,1},{1,2},{0,3},{7,4},{6,5},{5,6},{4,7},{11,8},{10,9},{9,1... | collective-permute-start | bytes 258056 | tf_op jit(solution)/shard_map/ppermute | solution.py:328
  10.9 0.0 collective-permute-start.1
  10.9 0.8 %collective-permute-start = (bf16[336,128]{1,0:T(8,128)(2,1)S(1)}, bf16[336,128]{1,0:T(8,128)(2,1)S(1)}, u32[]{:S(2)}, u32[]{:S(2)}) collective-permute-start(bf16[336,128]{1,0:T(8,128)(2,1)S(1)} %get-tuple-element.15.rest_0_), channel_id=1, source_target_pairs={{1,0},{0,1},{3,2},{2,3},{5,4},{4,5},{7,6},{6,7},{9,8},{8,9},{11,10... | collective-permute-start | bytes 258056 | tf_op jit(solution)/shard_map/ppermute | solution.py:328
  11.7 0.0 all-to-all-done
  11.7 2.2 %fetch_kernel.1 = bf16[32,32,128]{2,1,0:T(8,128)(2,1)} custom-call(bf16[32,16384]{1,0:T(8,128)(2,1)S(1)} %get-tuple-element.14.feats_ref, s32[1,1024]{1,0:T(1,128)S(1)} %bitcast.9), custom_call_target="tpu_custom_call" | custom-call | flops 1000000000 | bytes 1048576 | tf_op jit(solution)/shard_map/fetch_kernel/pallas_call | solution.py:337
  13.9 6.3 %all-to-all-start.1 = ((bf16[32,32,128]{2,1,0:T(8,128)(2,1)}), bf16[32,32,128]{2,1,0:T(8,128)(2,1)S(1)}, u32[]{:S(2)}, u32[]{:S(2)}) async-start(bf16[32,32,128]{2,1,0:T(8,128)(2,1)} %fetch_kernel.1), calls=%async_computation.1 | async-start | bytes 524288 | tf_op jit(solution)/shard_map/all_to_all | solution.py:338
  20.2 6.2 %late_kernel.1 = (f8e4m3fn[8,1024,256]{2,1,0:T(32,128)(4,1)S(1)}, f8e4m3fn[7,1024,256]{2,1,0:T(32,128)(4,1)}) custom-call(s32[10,15,256]{2,1,0:T(8,128)} %two_ref.1), custom_call_target="tpu_custom_call" | custom-call | flops 5000000000 | bytes 1048576 | tf_op jit(solution)/shard_map/late_kernel/pallas_call | solution.py:344
  26.5 0.0 copy-start
  26.5 0.0 copy-start.1
  26.5 0.0 collective-permute-done.2.rest_3_
  26.5 0.0 collective-permute-done.1.rest_2_
  26.5 0.0 collective-permute-done.rest_1_
  26.6 1.2 %prep_kernel.1 = (bf16[256,256]{1,0:T(8,128)(2,1)S(1)}, bf16[2,256,256]{2,1,0:T(8,128)(2,1)S(1)}, bf16[128,256]{1,0:T(8,128)(2,1)S(1)}, f32[256,128]{1,0:T(8,128)S(1)}, f32[256,128]{1,0:T(8,128)S(1)}) custom-call(bf16[256,128]{1,0:T(8,128)(2,1)} %w1s_ref.1, bf16[256,128]{1,0:T(8,128)(2,1)} %w1n_ref.1, bf16[336,128]{1,0:T(8,128)(2,1)S(1)} %get-tuple-element.15.rest_0_, ...), custom_call_target="tpu_custom_call" | custom-call | flops 1000000000 | bytes 1048576 | tf_op jit(solution)/shard_map/prep_kernel/pallas_call | solution.py:367
  27.8 2.7 %all-to-all-done.1 = bf16[32,32,128]{2,1,0:T(8,128)(2,1)S(1)} async-done(((bf16[32,32,128]{2,1,0:T(8,128)(2,1)}), bf16[32,32,128]{2,1,0:T(8,128)(2,1)S(1)}, u32[]{:S(2)}, u32[]{:S(2)}) %all-to-all-start.1) | async-done | bytes 262176 | tf_op jit(solution)/shard_map/all_to_all | solution.py:338
  30.5 0.0 copy-done
  30.5 0.0 copy-done.1
  30.5 5.0 %layer_kernel.1 = f32[64,256]{1,0:T(8,128)} custom-call(s32[1,8]{1,0:T(1,128)S(1)} %copy-done.1, bf16[8,128,128]{2,1,0:T(8,128)(2,1)S(1)} %bitcast.8, s32[15,256]{1,0:T(8,128)S(1)} %copy-done, bf16[256,256]{1,0:T(8,128)(2,1)S(1)} %get-tuple-element.16.w1, bf16[2,256,256]{2,1,0:T(8,128)(2,1)S(1)} %get-tuple-element.17.w2, ...), custom_call_target="tpu_custom_call" | custom-call | flops 5000000000 | bytes 1048576 | tf_op jit(solution)/shard_map/layer_kernel/pallas_call | solution.py:368
Async XLA Ops:
  0.0 11.7 %all-to-all-start = ((s32[1,8,128]{2,0,1:T(1,128)}), s32[1,8,128]{2,0,1:T(1,128)S(1)}, u32[]{:S(2)}, u32[]{:S(2)}) async-start(s32[1,8,128]{2,0,1:T(1,128)} %bitcast.10), calls=%async_computation | async-start | bytes 8192 | tf_op jit(solution)/shard_map/all_to_all | solution.py:309
  7.3 19.3 %collective-permute-start.2 = (bf16[336,128]{1,0:T(8,128)(2,1)S(1)}, bf16[336,128]{1,0:T(8,128)(2,1)S(1)}, u32[]{:S(2)}, u32[]{:S(2)}) collective-permute-start(bf16[336,128]{1,0:T(8,128)(2,1)S(1)} %get-tuple-element.15.rest_0_), channel_id=1, source_target_pairs={{3,0},{2,1},{1,2},{0,3},{7,4},{6,5},{5,6},{4,7},{11,8},{10,9},{9,1... | collective-permute-start | bytes 258056 | tf_op jit(solution)/shard_map/ppermute | solution.py:328
  10.9 15.6 %collective-permute-start.1 = (bf16[336,128]{1,0:T(8,128)(2,1)S(1)}, bf16[336,128]{1,0:T(8,128)(2,1)S(1)}, u32[]{:S(2)}, u32[]{:S(2)}) collective-permute-start(bf16[336,128]{1,0:T(8,128)(2,1)S(1)} %get-tuple-element.15.rest_0_), channel_id=1, source_target_pairs={{2,0},{3,1},{0,2},{1,3},{6,4},{7,5},{4,6},{5,7},{10,8},{11,9},{8,1... | collective-permute-start | bytes 258056 | tf_op jit(solution)/shard_map/ppermute | solution.py:328
  10.9 15.6 %collective-permute-start = (bf16[336,128]{1,0:T(8,128)(2,1)S(1)}, bf16[336,128]{1,0:T(8,128)(2,1)S(1)}, u32[]{:S(2)}, u32[]{:S(2)}) collective-permute-start(bf16[336,128]{1,0:T(8,128)(2,1)S(1)} %get-tuple-element.15.rest_0_), channel_id=1, source_target_pairs={{1,0},{0,1},{3,2},{2,3},{5,4},{4,5},{7,6},{6,7},{9,8},{8,9},{11,10... | collective-permute-start | bytes 258056 | tf_op jit(solution)/shard_map/ppermute | solution.py:328
  13.9 16.6 %all-to-all-start.1 = ((bf16[32,32,128]{2,1,0:T(8,128)(2,1)}), bf16[32,32,128]{2,1,0:T(8,128)(2,1)S(1)}, u32[]{:S(2)}, u32[]{:S(2)}) async-start(bf16[32,32,128]{2,1,0:T(8,128)(2,1)} %fetch_kernel.1), calls=%async_computation.1 | async-start | bytes 524288 | tf_op jit(solution)/shard_map/all_to_all | solution.py:338
  26.5 4.0 %copy-start = (s32[15,256]{1,0:T(8,128)S(1)}, s32[15,256]{1,0:T(8,128)}, u32[]{:S(2)}) copy-start(s32[15,256]{1,0:T(8,128)} %one_ref.1) | copy-start | bytes 46084
  26.5 4.0 %copy-start.1 = (s32[1,8]{1,0:T(1,128)S(1)}, s32[1,8]{1,0:T(1,128)}, u32[]{:S(2)}) copy-start(s32[1,8]{1,0:T(1,128)} %live_ref.1) | copy-start | bytes 100

commit v5 on v4

--- a/solution.py
+++ b/solution.py
@@ -38,9 +38,9 @@
 
 def pick_columns(feats_ref, rows, emit, ready=None):
     feat_dev, nodes = feats_ref.shape
-    group = max(1, min(256 // feat_dev, nodes // LANES))
-    for start in range(0, rows.shape[1], LANES):
-        want = rows[:, start : start + LANES]
+    group = max(1, min(128 // feat_dev, nodes // LANES))
+    for start in range(0, rows.shape[1], 2 * LANES):
+        want = rows[:, start : start + 2 * LANES]
         width = want.shape[1]
         high = want >> 8
         low = want & (LANES - 1)

time: 35.8 us -> 35.7 us (level)
  no operation moved by 1% of the time
where the time goes in v5:
time: 35.7 us; the launch traced here: 35.4 us
  Pallas kernels  16.6 us (46%)
  starting transfers between devices  16 us (45%)
  waiting for transfers between devices  2.73 us (8%)
    all_to_all x1, starting transfers between devices, per_device(): lax.all_to_all(served, ('dom', 'feat'), split_axis=0, concat_axis=0, tile...  6.32 us
    pallas_call x1, Pallas kernels, per_device(): pl.pallas_call(functools.partial(late_kernel, held), out_shape=[pltpu.VME...  6.24 us
    all_to_all x1, starting transfers between devices, per_device(): lax.all_to_all(want_rows, 'dom', split_axis=1, concat_axis=0, tiled=True)  5.2 us
    pallas_call x1, Pallas kernels, per_device(): pl.pallas_call(functools.partial(layer_kernel, fan_two), out_shape=jax.Sh...  5 us
    ppermute x3, starting transfers between devices, per_device(): pieces.append(lax.ppermute(mine, 'feat', pairs))  4.45 us
    all_to_all x1, waiting for transfers between devices, per_device(): lax.all_to_all(served, ('dom', 'feat'), split_axis=0, concat_axis=0, tile...  2.72 us
    pallas_call x1, Pallas kernels, per_device(): served = fetch(near, asked.reshape(1, slots))  2.11 us
    pallas_call x1, Pallas kernels, per_device(): pl.pallas_call(early_kernel, out_shape=[pltpu.VMEM((rows, 128), BF16), pl...  2.06 us
  transfers between devices with their start and end apart: 5, of which 1 were waited for; matrix products, arithmetic and copies ran while one was open for 0% of the time, Pallas kernels for 33%

profile of v5, /device:TPU:0, one launch (start us, length us, event | category | flops | bytes accessed | tf_op | source)
XLA Modules:
  0.0 35.4 jit_solution(11687815820961237284)
XLA Ops:
  0.0 5.2 %all-to-all-start = ((s32[1,8,128]{2,0,1:T(1,128)}), s32[1,8,128]{2,0,1:T(1,128)S(1)}, u32[]{:S(2)}, u32[]{:S(2)}) async-start(s32[1,8,128]{2,0,1:T(1,128)} %bitcast.10), calls=%async_computation | async-start | bytes 8192 | tf_op jit(solution)/shard_map/all_to_all | solution.py:309
  5.2 2.1 %early_kernel.1 = (bf16[336,128]{1,0:T(8,128)(2,1)S(1)}, bf16[32,16384]{1,0:T(8,128)(2,1)S(1)}) custom-call(bf16[32,16384]{1,0:T(8,128)(2,1)} %feats_ref.1, s32[1,256]{1,0:T(1,128)} %bitcast.13, bf16[64,256]{1,0:T(8,128)(2,1)} %bitcast.11, bf16[64,256]{1,0:T(8,128)(2,1)} %bitcast.12, f32[1,64]{1,0:T(1,128)} %bitcast.14, f32[1,64]{1,0:T(1,128)} %bitcast.15), custom_call_target="tpu_custom_call" | custom-call | flops 1000000000 | bytes 1048576 | tf_op jit(solution)/shard_map/early_kernel/pallas_call | solution.py:315
  7.3 3.7 %collective-permute-start.2 = (bf16[336,128]{1,0:T(8,128)(2,1)S(1)}, bf16[336,128]{1,0:T(8,128)(2,1)S(1)}, u32[]{:S(2)}, u32[]{:S(2)}) collective-permute-start(bf16[336,128]{1,0:T(8,128)(2,1)S(1)} %get-tuple-element.15.rest_0_), channel_id=1, source_target_pairs={{3,0},{2,1},{1,2},{0,3},{7,4},{6,5},{5,6},{4,7},{11,8},{10,9},{9,1... | collective-permute-start | bytes 258056 | tf_op jit(solution)/shard_map/ppermute | solution.py:328
  10.9 0.0 collective-permute-start.1
  10.9 0.8 %collective-permute-start = (bf16[336,128]{1,0:T(8,128)(2,1)S(1)}, bf16[336,128]{1,0:T(8,128)(2,1)S(1)}, u32[]{:S(2)}, u32[]{:S(2)}) collective-permute-start(bf16[336,128]{1,0:T(8,128)(2,1)S(1)} %get-tuple-element.15.rest_0_), channel_id=1, source_target_pairs={{1,0},{0,1},{3,2},{2,3},{5,4},{4,5},{7,6},{6,7},{9,8},{8,9},{11,10... | collective-permute-start | bytes 258056 | tf_op jit(solution)/shard_map/ppermute | solution.py:328
  11.7 0.0 all-to-all-done
  11.7 2.1 %fetch_kernel.1 = bf16[32,32,128]{2,1,0:T(8,128)(2,1)} custom-call(bf16[32,16384]{1,0:T(8,128)(2,1)S(1)} %get-tuple-element.14.feats_ref, s32[1,1024]{1,0:T(1,128)S(1)} %bitcast.9), custom_call_target="tpu_custom_call" | custom-call | flops 1000000000 | bytes 1048576 | tf_op jit(solution)/shard_map/fetch_kernel/pallas_call | solution.py:337
  13.8 6.3 %all-to-all-start.1 = ((bf16[32,32,128]{2,1,0:T(8,128)(2,1)}), bf16[32,32,128]{2,1,0:T(8,128)(2,1)S(1)}, u32[]{:S(2)}, u32[]{:S(2)}) async-start(bf16[32,32,128]{2,1,0:T(8,128)(2,1)} %fetch_kernel.1), calls=%async_computation.1 | async-start | bytes 524288 | tf_op jit(solution)/shard_map/all_to_all | solution.py:338
  20.2 6.2 %late_kernel.1 = (f8e4m3fn[8,1024,256]{2,1,0:T(32,128)(4,1)S(1)}, f8e4m3fn[7,1024,256]{2,1,0:T(32,128)(4,1)}) custom-call(s32[10,15,256]{2,1,0:T(8,128)} %two_ref.1), custom_call_target="tpu_custom_call" | custom-call | flops 5000000000 | bytes 1048576 | tf_op jit(solution)/shard_map/late_kernel/pallas_call | solution.py:344
  26.4 0.0 copy-start
  26.4 0.0 copy-start.1
  26.4 0.0 collective-permute-done.2.rest_3_
  26.4 0.0 collective-permute-done.1.rest_2_
  26.5 0.0 collective-permute-done.rest_1_
  26.5 1.2 %prep_kernel.1 = (bf16[256,256]{1,0:T(8,128)(2,1)S(1)}, bf16[2,256,256]{2,1,0:T(8,128)(2,1)S(1)}, bf16[128,256]{1,0:T(8,128)(2,1)S(1)}, f32[256,128]{1,0:T(8,128)S(1)}, f32[256,128]{1,0:T(8,128)S(1)}) custom-call(bf16[256,128]{1,0:T(8,128)(2,1)} %w1s_ref.1, bf16[256,128]{1,0:T(8,128)(2,1)} %w1n_ref.1, bf16[336,128]{1,0:T(8,128)(2,1)S(1)} %get-tuple-element.15.rest_0_, ...), custom_call_target="tpu_custom_call" | custom-call | flops 1000000000 | bytes 1048576 | tf_op jit(solution)/shard_map/prep_kernel/pallas_call | solution.py:367
  27.7 2.7 %all-to-all-done.1 = bf16[32,32,128]{2,1,0:T(8,128)(2,1)S(1)} async-done(((bf16[32,32,128]{2,1,0:T(8,128)(2,1)}), bf16[32,32,128]{2,1,0:T(8,128)(2,1)S(1)}, u32[]{:S(2)}, u32[]{:S(2)}) %all-to-all-start.1) | async-done | bytes 262176 | tf_op jit(solution)/shard_map/all_to_all | solution.py:338
  30.4 0.0 copy-done
  30.4 0.0 copy-done.1
  30.4 5.0 %layer_kernel.1 = f32[64,256]{1,0:T(8,128)} custom-call(s32[1,8]{1,0:T(1,128)S(1)} %copy-done.1, bf16[8,128,128]{2,1,0:T(8,128)(2,1)S(1)} %bitcast.8, s32[15,256]{1,0:T(8,128)S(1)} %copy-done, bf16[256,256]{1,0:T(8,128)(2,1)S(1)} %get-tuple-element.16.w1, bf16[2,256,256]{2,1,0:T(8,128)(2,1)S(1)} %get-tuple-element.17.w2, ...), custom_call_target="tpu_custom_call" | custom-call | flops 5000000000 | bytes 1048576 | tf_op jit(solution)/shard_map/layer_kernel/pallas_call | solution.py:368
Async XLA Ops:
  0.0 11.7 %all-to-all-start = ((s32[1,8,128]{2,0,1:T(1,128)}), s32[1,8,128]{2,0,1:T(1,128)S(1)}, u32[]{:S(2)}, u32[]{:S(2)}) async-start(s32[1,8,128]{2,0,1:T(1,128)} %bitcast.10), calls=%async_computation | async-start | bytes 8192 | tf_op jit(solution)/shard_map/all_to_all | solution.py:309
  7.3 19.2 %collective-permute-start.2 = (bf16[336,128]{1,0:T(8,128)(2,1)S(1)}, bf16[336,128]{1,0:T(8,128)(2,1)S(1)}, u32[]{:S(2)}, u32[]{:S(2)}) collective-permute-start(bf16[336,128]{1,0:T(8,128)(2,1)S(1)} %get-tuple-element.15.rest_0_), channel_id=1, source_target_pairs={{3,0},{2,1},{1,2},{0,3},{7,4},{6,5},{5,6},{4,7},{11,8},{10,9},{9,1... | collective-permute-start | bytes 258056 | tf_op jit(solution)/shard_map/ppermute | solution.py:328
  10.9 15.5 %collective-permute-start.1 = (bf16[336,128]{1,0:T(8,128)(2,1)S(1)}, bf16[336,128]{1,0:T(8,128)(2,1)S(1)}, u32[]{:S(2)}, u32[]{:S(2)}) collective-permute-start(bf16[336,128]{1,0:T(8,128)(2,1)S(1)} %get-tuple-element.15.rest_0_), channel_id=1, source_target_pairs={{2,0},{3,1},{0,2},{1,3},{6,4},{7,5},{4,6},{5,7},{10,8},{11,9},{8,1... | collective-permute-start | bytes 258056 | tf_op jit(solution)/shard_map/ppermute | solution.py:328
  10.9 15.5 %collective-permute-start = (bf16[336,128]{1,0:T(8,128)(2,1)S(1)}, bf16[336,128]{1,0:T(8,128)(2,1)S(1)}, u32[]{:S(2)}, u32[]{:S(2)}) collective-permute-start(bf16[336,128]{1,0:T(8,128)(2,1)S(1)} %get-tuple-element.15.rest_0_), channel_id=1, source_target_pairs={{1,0},{0,1},{3,2},{2,3},{5,4},{4,5},{7,6},{6,7},{9,8},{8,9},{11,10... | collective-permute-start | bytes 258056 | tf_op jit(solution)/shard_map/ppermute | solution.py:328
  13.8 16.6 %all-to-all-start.1 = ((bf16[32,32,128]{2,1,0:T(8,128)(2,1)}), bf16[32,32,128]{2,1,0:T(8,128)(2,1)S(1)}, u32[]{:S(2)}, u32[]{:S(2)}) async-start(bf16[32,32,128]{2,1,0:T(8,128)(2,1)} %fetch_kernel.1), calls=%async_computation.1 | async-start | bytes 524288 | tf_op jit(solution)/shard_map/all_to_all | solution.py:338
  26.4 4.0 %copy-start = (s32[15,256]{1,0:T(8,128)S(1)}, s32[15,256]{1,0:T(8,128)}, u32[]{:S(2)}) copy-start(s32[15,256]{1,0:T(8,128)} %one_ref.1) | copy-start | bytes 46084
  26.4 4.0 %copy-start.1 = (s32[1,8]{1,0:T(1,128)S(1)}, s32[1,8]{1,0:T(1,128)}, u32[]{:S(2)}) copy-start(s32[1,8]{1,0:T(1,128)} %live_ref.1) | copy-start | bytes 100
